TPU v7x, 256 devices: a whole 4x4x8 slice. The times are simulated.
256 devices in a mesh: row: 16 (over z_lo, y, core), col: 16 (over z_hi, x).
Axes of the slice: x: 4, y: 4, z: 8 (z_hi: 4, z_lo: 2; z = z_hi * 2 + z_lo), core: 2. Of those that a mesh axis runs over, the one named last changes fastest.
Arguments:
- tokens: bfloat16 [256, 2, 4096], P(None, None, 'row'), may hold values from -6 to 6
- task_emb: bfloat16 [512, 1024], replicated, may hold values from -6 to 6
- gen_in: bfloat16 [1024, 512], replicated, may hold values from -0.1875 to 0.1875
- gen_a: bfloat16 [512, 4096, 16], P(None, ('row', 'col')), may hold values from -0.0078125 to 0.0078125
- gen_b: bfloat16 [512, 16, 14336], P(None, 'row', 'col'), may hold values from -0.125 to 0.125
- w_gate: bfloat16 [4096, 14336], P('row', 'col'), may hold values from -0.09375 to 0.09375
- w_up: bfloat16 [4096, 14336], P('row', 'col'), may hold values from -0.09375 to 0.09375
- w_down: bfloat16 [14336, 4096], P('col', 'row'), may hold values from -0.046875 to 0.046875
- group_count: int32 [64], replicated, may hold values from 1 to 16, 256 in all
- group_task: int32 [64], replicated, may hold values from 0 to 511, as said below
Outputs:
- mixed: bfloat16 [256, 2, 4096], P('col', None, 'row')
Inputs may be any that keep to these rules, and one draw needn't show every extreme that they name: `group_count`: requests in each group, in the order of the requests; they sum to 256 and the largest is 16. `group_task`: distinct task ids, one for each group.
All inputs are finite; a program needn't handle non-finite values.
Results may differ from a plain program's by a relative error of at most 0.0078.
Values may be sent and summed in bfloat16 or wider, within the bound.
A program may use at most 64 MiB of HBM per device.

v0:
```python
import jax
import jax.numpy as jnp
from jax import lax
from jax.sharding import Mesh
from jax.sharding import PartitionSpec as P

ROW = ("row_0", "row_1", "row_2")
ROW_COL = ("row_0", "row_1", "row_2", "col")


def laid_out(tiles, dim):
    dims = list(tiles.shape[1:])
    dims[dim] *= tiles.shape[0]
    return jnp.moveaxis(tiles, 0, dim).reshape(dims)


def from_everyone(value, axis):
    peers = lax.axis_size(axis)
    return lax.all_to_all(
        jnp.broadcast_to(value[None], (peers, *value.shape)), axis, 0, 0, tiled=True
    )


def collect(value, axis, dim):
    return laid_out(from_everyone(value, axis), dim)


def in_blocks(value, dim, peers):
    before, after = (value.shape[:dim], value.shape[dim + 1 :])
    return jnp.moveaxis(value.reshape(*before, peers, -1, *after), dim, 0)


def sum_at_owner(value, axis, dim):
    peers = lax.axis_size(axis)
    tiles = lax.all_to_all(in_blocks(value, dim, peers), axis, 0, 0, tiled=True)
    return jnp.sum(tiles, axis=0)


def sum_by_axis(value, axes, dim):
    far, near = axes
    own = sum_at_owner(in_blocks(value, dim, lax.axis_size(far)), near, dim + 1)
    return jnp.sum(lax.all_to_all(own, far, 0, 0, tiled=True), axis=0)


def in_one_piece(arrays, axis, dim, along):
    widths = [a.shape[along] for a in arrays]
    both = jnp.concatenate(arrays, axis=along)
    out = sum_by_axis(both, axis, dim)
    return tuple(jnp.split(out, [sum(widths[:k]) for k in range(1, len(widths))], axis=along))


def shards(tokens, task_emb, gen_in, gen_a, gen_b, w_gate, w_up, w_down, group_count, group_task):
    batch_size, draft_len, width_part = tokens.shape
    row_count = batch_size * draft_len
    flat_tokens = tokens.reshape(row_count, width_part)
    groups = group_count.shape[0]
    group_ends = jnp.cumsum(group_count)
    group_starts = group_ends - group_count
    request_ids = jnp.arange(batch_size, dtype=jnp.int32)
    membership = (request_ids[:, None] >= group_starts[None, :]) & (
        request_ids[:, None] < group_ends[None, :]
    )
    member_rows = jnp.repeat(membership, draft_len, axis=0)
    member_float = member_rows.astype(jnp.float32)
    member_half = member_rows.astype(jnp.bfloat16)
    chosen = jnp.take(task_emb, group_task, axis=0)
    hyper_out = jax.nn.silu(jnp.dot(chosen, gen_in, preferred_element_type=jnp.float32)).astype(
        jnp.bfloat16
    )
    hyper_width, slab_width, rank_dim = gen_a.shape
    a_local = jnp.dot(
        hyper_out,
        gen_a.reshape(hyper_width, slab_width * rank_dim),
        preferred_element_type=jnp.float32,
    )
    a_local = a_local.astype(jnp.bfloat16).reshape(groups, slab_width, rank_dim)
    a_local = a_local.transpose(1, 0, 2).reshape(slab_width, groups * rank_dim)
    wide_low = jnp.dot(flat_tokens, collect(a_local, "col", 0), preferred_element_type=jnp.float32)
    low_part = jnp.sum(
        wide_low.reshape(row_count, groups, rank_dim) * member_float[:, :, None], axis=1
    )
    gate_part = jnp.dot(flat_tokens, w_gate, preferred_element_type=jnp.float32)
    up_part = jnp.dot(flat_tokens, w_up, preferred_element_type=jnp.float32)
    _, rank_part, ff_part = gen_b.shape
    b_local = jnp.dot(
        hyper_out,
        gen_b.reshape(hyper_width, rank_part * ff_part),
        preferred_element_type=jnp.float32,
    )
    b_local = b_local.astype(jnp.bfloat16).reshape(groups, rank_part, ff_part)
    gate_total, up_total, low_sum = in_one_piece(
        (gate_part, up_part, low_part), (("row_0", "row_1"), "row_2"), 0, 1
    )
    share_rows = row_count // lax.axis_size(ROW)
    member_share = lax.dynamic_slice_in_dim(
        member_half, lax.axis_index(ROW) * share_rows, share_rows, 0
    )
    low_half = low_sum.astype(jnp.bfloat16)
    spread = member_share[:, :, None] * low_half[:, None, :]
    share_rows = spread.shape[0]
    block_piece = lax.all_gather(b_local, ROW, axis=1, tiled=True)
    ranks_here = block_piece.shape[1]
    picked = spread.reshape(share_rows, groups * ranks_here)
    adapter_update = jnp.dot(
        picked,
        block_piece.reshape(groups * ranks_here, ff_part),
        preferred_element_type=jnp.float32,
    )
    hidden_share = (jax.nn.silu(gate_total) * (up_total + adapter_update)).astype(jnp.bfloat16)
    hidden_state = collect(hidden_share, ROW, 0)
    col_count = lax.axis_size("col")
    picked = hidden_state
    mixed = sum_at_owner(jnp.dot(picked, w_down, preferred_element_type=jnp.float32), "col", 0)
    return mixed.astype(jnp.bfloat16).reshape(batch_size // col_count, draft_len, w_down.shape[1])


def solution(mesh):
    split = Mesh(
        mesh.devices.reshape(2, 4, 2, mesh.shape["col"]), ("row_0", "row_1", "row_2", "col")
    )
    placed = (
        P(None, None, ROW),
        P(),
        P(),
        P(None, ROW_COL, None),
        P(None, ROW, "col"),
        P(ROW, "col"),
        P(ROW, "col"),
        P("col", ROW),
        P(),
        P(),
    )
    return jax.shard_map(
        shards, mesh=split, in_specs=placed, out_specs=P("col", None, ROW), check_vma=False
    )
```

profile of v0, /device:TPU:32, one launch (start us, length us, event | category | flops | bytes accessed | tf_op | source)
XLA Modules:
  0.0 137.4 jit_solution(9935942233922256284)
XLA Ops:
  6.5 0.0 copy-start
  6.5 0.0 copy-start.3
  6.5 0.8 compare_select_fusion
  7.3 0.7 compare_and_fusion
  8.0 0.0 copy-done
  8.0 0.7 gather_fusion
  8.7 0.0 copy-start.1
  8.7 1.7 %multiply_convert_fusion = bf16[64,512]{1,0:T(8,128)(2,1)S(1)} fusion(bf16[1024,512]{1,0:T(8,128)(2,1)} %param.12, bf16[64,1024]{1,0:T(8,128)(2,1)S(1)} %gather_fusion, pred[64]{0:T(512)(128)(4,1)S(1)} %compare_and_fusion), kind=kOutput, calls=%fused_computation.18 | convolution fusion | flops 67338240 | bytes 1245248 | tf_op jit(solution)/shard_map/dot_general | solution.py:67
  10.4 0.0 copy-start.5
  10.4 0.0 copy-start.4
  10.4 0.0 copy-done.3
  10.4 0.2 convolution_convert_fusion.1
  10.6 0.1 copy.33
  10.7 0.2 copy.34
  10.9 0.3 broadcast_in_dim.40
  11.2 0.9 broadcast_in_dim.41
  12.1 10.2 %all-to-all-start = ((bf16[16,16,1024]{2,1,0:T(8,128)(2,1)}), bf16[16,16,1024]{2,1,0:T(8,128)(2,1)}, u32[]{:S(2)}, u32[]{:S(2)}) async-start(bf16[16,16,1024]{2,1,0:T(8,128)(2,1)} %broadcast_in_dim.41), calls=%async_computation | async-start | bytes 1048576 | tf_op jit(solution)/shard_map/all_to_all | solution.py:19
  22.3 0.0 all-gather.3.cloned.1.call-start
  22.4 0.0 copy-done.1
  22.4 0.9 convolution_convert_fusion
  23.3 0.0 all-gather.3.cloned.1.call-update
  23.3 0.0 copy-done.5
  23.3 0.1 copy.35
  23.4 0.1 reduce-window.8
  23.5 0.1 reduce
  23.7 0.0 copy-done.4
  23.7 0.1 reshape.71
  23.8 0.1 broadcast_in_dim.42
  23.9 0.1 copy.36
  24.0 1.5 %fusion.19 = f32[512,896]{1,0:T(8,128)S(1)} fusion(bf16[512,256]{1,0:T(8,128)(2,1)S(1)} %reshape.71, bf16[256,896]{1,0:T(8,128)(2,1)} %param.15), kind=kOutput, calls=%fused_computation.32 | convolution fusion | flops 234881024 | bytes 2555904 | tf_op jit(solution)/shard_map/dot_general | solution.py:82
  25.5 2.7 %fusion.20 = f32[512,896]{1,0:T(8,128)} fusion(bf16[512,256]{1,0:T(8,128)(2,1)S(1)} %reshape.71, bf16[256,896]{1,0:T(8,128)(2,1)} %param.16), kind=kOutput, calls=%fused_computation.33 | convolution fusion | flops 234881024 | bytes 2555904 | tf_op jit(solution)/shard_map/dot_general | solution.py:83
  28.2 11.6 %all-to-all-done = bf16[16,16,1024]{2,1,0:T(8,128)(2,1)} async-done(((bf16[16,16,1024]{2,1,0:T(8,128)(2,1)}), bf16[16,16,1024]{2,1,0:T(8,128)(2,1)}, u32[]{:S(2)}, u32[]{:S(2)}) %all-to-all-start) | async-done | bytes 524320 | tf_op jit(solution)/shard_map/all_to_all | solution.py:19
  39.8 1.5 %fusion.21 = f32[1024,512]{1,0:T(8,128)S(1)} fusion(bf16[256,1024]{1,0:T(8,128)(2,1)} %bitcast.3, bf16[512,256]{1,0:T(8,128)(2,1)S(1)} %reshape.71), kind=kOutput, calls=%fused_computation.34 | convolution fusion | flops 268435456 | bytes 2883584 | tf_op jit(solution)/shard_map/dot_general | solution.py:78
  41.3 0.4 multiply_reduce_fusion
  41.7 0.1 copy.37
  41.8 1.8 %pad_maximum_fusion = f32[512,1808]{1,0:T(8,128)S(1)} fusion(f32[512,16]{1,0:T(8,128)S(1)} %copy.37, f32[512,896]{1,0:T(8,128)} %fusion.20, f32[512,896]{1,0:T(8,128)S(1)} %fusion.19), kind=kLoop, calls=%fused_computation.1 | loop fusion | flops 1851392 | bytes 7405568 | tf_op jit(solution)/shard_map/concatenate | solution.py:47
  43.7 0.3 copy.43
  43.9 8.1 %all_to_all.25 = f32[2,8,32,1808]{3,2,1,0:T(8,128)} all-to-all(f32[2,8,32,1808]{3,2,1,0:T(8,128)S(1)} %bitcast.44), channel_id=1, replica_groups=mesh['row_0'=2,'row_1'=4,'row_2'=2,'col'=16] {'row_2'}, dimensions={0} | all-to-all | bytes 7405568 | tf_op jit(solution)/shard_map/all_to_all | solution.py:35
  52.0 3.9 %reduce_sum.37 = f32[8,32,1808]{2,1,0:T(8,128)} reduce(f32[2,8,32,1808]{3,2,1,0:T(8,128)} %all_to_all.25, f32[]{:T(128)} %constant.41.clone.1), dimensions={0}, to_apply=%region_2.3 | reduce | flops 462848 | bytes 5554180 | tf_op jit(solution)/shard_map/reduce_sum | solution.py:36
  55.9 5.9 %all-to-all-start.2 = ((f32[8,32,1808]{2,1,0:T(8,128)}), f32[8,32,1808]{2,1,0:T(8,128)S(1)}, u32[]{:S(2)}, u32[]{:S(2)}) async-start(f32[8,32,1808]{2,1,0:T(8,128)} %reduce_sum.37), calls=%async_computation.2 | async-start | bytes 3932160 | tf_op jit(solution)/shard_map/all_to_all | solution.py:42
  61.8 0.1 broadcast_in_dim.43
  61.9 0.1 copy.39
  62.0 0.4 all-gather.3.cloned.1.call-done
  62.4 3.0 %copy.41 = bf16[8,8,16,896]{3,2,1,0:T(8,128)(2,1)} copy(bf16[8,8,16,896]{3,1,2,0:T(8,128)(2,1)} %bitcast.47) | data formatting | bytes 3670016
  65.4 20.8 %all-to-all-done.2 = f32[8,32,1808]{2,1,0:T(8,128)S(1)} async-done(((f32[8,32,1808]{2,1,0:T(8,128)}), f32[8,32,1808]{2,1,0:T(8,128)S(1)}, u32[]{:S(2)}, u32[]{:S(2)}) %all-to-all-start.2) | async-done | bytes 1851424 | tf_op jit(solution)/shard_map/all_to_all | solution.py:42
  86.3 0.1 reduce_sum.38
  86.4 0.1 copy.40
  86.5 0.0 copy-start.2
  86.5 2.0 %fusion.2 = bf16[32,896]{1,0:T(8,128)(2,1)S(1)} fusion(bf16[64,16,896]{2,1,0:T(8,128)(2,1)} %bitcast.46, bf16[32,16]{0,1:T(8,128)(2,1)S(1)} %copy.40, bf16[32,64]{0,1:T(8,128)(2,1)S(1)} %copy.39, f32[32,1808]{1,0:T(8,128)S(1)} %reduce_sum.38), kind=kOutput, calls=%fused_computation.8 | convolution fusion | flops 58953728 | bytes 2126848 | tf_op jit(solution)/shard_map/dot_general | solution.py:104
  88.5 0.1 broadcast_in_dim.44
  88.5 17.7 %all_to_all.26 = bf16[16,32,896]{2,1,0:T(8,128)(2,1)S(1)} all-to-all(bf16[16,32,896]{2,1,0:T(8,128)(2,1)S(1)} %broadcast_in_dim.44), channel_id=1, replica_groups=mesh['row_0'=2,'row_1'=4,'row_2'=2,'col'=16] {'row_0','row_1','row_2'}, dimensions={0} | all-to-all | bytes 1835008 | tf_op jit(solution)/shard_map/all_to_all | solution.py:19
  106.2 0.0 copy-done.2
  106.2 0.4 fusion.4
  106.7 23.3 %all_to_all.27 = f32[16,32,256]{2,1,0:T(8,128)S(1)} all-to-all(f32[16,32,256]{2,1,0:T(8,128)S(1)} %fusion.4), channel_id=1, replica_groups=mesh['row_0'=2,'row_1'=4,'row_2'=2,'col'=16] {'col'}, dimensions={0} | all-to-all | bytes 1048576 | tf_op jit(solution)/shard_map/all_to_all | solution.py:35
  130.0 0.6 convert_element_type.47
  (6 shorter events, 0.1 us)
Async XLA Ops:
  6.5 1.4 %copy-start = (bf16[512,1024]{1,0:T(8,128)(2,1)S(1)}, bf16[512,1024]{1,0:T(8,128)(2,1)}, u32[]{:S(2)}) copy-start(bf16[512,1024]{1,0:T(8,128)(2,1)} %param.11) | copy-start | bytes 3145732
  6.5 3.9 %copy-start.3 = (bf16[512,16,16]{0,2,1:T(8,128)(2,1)S(1)}, bf16[512,16,16]{0,2,1:T(8,128)(2,1)}, u32[]{:S(2)}) copy-start(bf16[512,16,16]{0,2,1:T(8,128)(2,1)} %param.13) | copy-start | bytes 786436
  8.7 13.7 %copy-start.1 = (bf16[512,1,896]{2,0,1:T(8,128)(2,1)S(1)}, bf16[512,1,896]{2,0,1:T(8,128)(2,1)}, u32[]{:S(2)}) copy-start(bf16[512,1,896]{2,0,1:T(8,128)(2,1)} %param.14) | copy-start | bytes 2752516
  10.4 12.9 %copy-start.5 = (s32[64]{0:T(128)S(1)}, s32[64]{0:T(128)}, u32[]{:S(2)}) copy-start(s32[64]{0:T(128)} %param.18) | copy-start | bytes 772
  10.4 13.3 %copy-start.4 = (bf16[256,2,256]{2,1,0:T(2,128)(2,1)S(1)}, bf16[256,2,256]{2,1,0:T(2,128)(2,1)}, u32[]{:S(2)}) copy-start(bf16[256,2,256]{2,1,0:T(2,128)(2,1)} %param.10) | copy-start | bytes 786436
  12.1 27.6 %all-to-all-start = ((bf16[16,16,1024]{2,1,0:T(8,128)(2,1)}), bf16[16,16,1024]{2,1,0:T(8,128)(2,1)}, u32[]{:S(2)}, u32[]{:S(2)}) async-start(bf16[16,16,1024]{2,1,0:T(8,128)(2,1)} %broadcast_in_dim.41), calls=%async_computation | async-start | bytes 1048576 | tf_op jit(solution)/shard_map/all_to_all | solution.py:19
  22.3 40.1 %all-gather.3.cloned.1.call-start = ((), (), s32[]{:S(2)}) async-start(), calls=%async_computation.5 | async-start | bytes 1949696 | tf_op jit(solution)/shard_map/all_gather | solution.py:101
  55.9 30.3 %all-to-all-start.2 = ((f32[8,32,1808]{2,1,0:T(8,128)}), f32[8,32,1808]{2,1,0:T(8,128)S(1)}, u32[]{:S(2)}, u32[]{:S(2)}) async-start(f32[8,32,1808]{2,1,0:T(8,128)} %reduce_sum.37), calls=%async_computation.2 | async-start | bytes 3932160 | tf_op jit(solution)/shard_map/all_to_all | solution.py:42
  86.5 19.8 %copy-start.2 = (bf16[896,256]{1,0:T(8,128)(2,1)S(1)}, bf16[896,256]{1,0:T(8,128)(2,1)}, u32[]{:S(2)}) copy-start(bf16[896,256]{1,0:T(8,128)(2,1)} %param.17) | copy-start | bytes 1376260
Sparse Core Ops, SparseCore 0:
  24.9 37.4 all-gather.2
where the time goes:
time: 138 us; the launch traced here: 137 us
  blocking collectives  49.1 us (36%)
  waiting for transfers between devices  32.8 us (24%)
  starting transfers between devices  16.1 us (12%)
  between operations  13.6 us (10%)
  matrix products  10.9 us (8%)
  other arithmetic  7.93 us (6%)
  local copies, waits for them, and re-layouts  6.97 us (5%)
    all_to_all x2, blocking collectives, sum_at_owner(): tiles = lax.all_to_all(in_blocks(value, dim, peers), axis, 0, 0, tiled=True)  31.4 us
    all_to_all x1, waiting for transfers between devices, sum_by_axis(): return jnp.sum(lax.all_to_all(own, far, 0, 0, tiled=True), axis=0)  20.8 us
    all_to_all x1, blocking collectives, from_everyone(): lax.all_to_all(jnp.broadcast_to(value[None], (peers, *value.shape)), axis...  17.7 us
    all_to_all x1, waiting for transfers between devices, from_everyone(): lax.all_to_all(jnp.broadcast_to(value[None], (peers, *value.shape)), axis...  11.6 us
    all_to_all x1, starting transfers between devices, from_everyone(): lax.all_to_all(jnp.broadcast_to(value[None], (peers, *value.shape)), axis...  10.2 us
    all_to_all x1, starting transfers between devices, sum_by_axis(): return jnp.sum(lax.all_to_all(own, far, 0, 0, tiled=True), axis=0)  5.92 us
    reduce_sum x2, other arithmetic, sum_at_owner(): return jnp.sum(tiles, axis=0)  3.92 us
    unnamed x13, local copies, waits for them, and re-layouts  3.03 us
  transfers between devices with their start and end apart: 3, of which 3 were waited for; matrix products, arithmetic and copies ran while one was open for 12% of the time, Pallas kernels for 0%

commit v1 on v0

v1 whole, which is shorter than its diff:
```python
import functools

import jax
import jax.numpy as jnp
from jax import lax
from jax.experimental import pallas as pl
from jax.experimental.pallas import tpu as pltpu
from jax.sharding import PartitionSpec as P

MESH = pl.DeviceIdType.MESH
F32 = jnp.float32
BF16 = jnp.bfloat16


def dot(a, b, dims=((1,), (0,))):
    return lax.dot_general(a, b, (dims, ((), ())), preferred_element_type=F32)


def kernel(
    tokens, task_emb, gen_in, gen_a, gen_b, w_gate, w_up, w_down, count, task,
    out,
    tok_v, emb_v, gin_v, ga_v, gb_v, wg_v, wu_v, wd_v, cnt_v, tsk_v,
    tokp_v, wgp_v, wup_v, wdp_v, b_v,
    low_s, low1_r, low1_s, low2_r,
    gate_s, up_s, gate_r, up_r, hid_v, mix_own, mix_par, mix_r,
    load_sem, pair_ss, pair_rs, l1_ss, l1_rs, l2_ss, l2_rs,
    g_ss, g_rs, u_ss, u_rs, h_ss, h_rs, m_ss, m_rs,
):
    row = lax.axis_index("row")
    col = lax.axis_index("col")
    chip = row // 2
    core = row % 2
    groups = count.shape[1]
    ranks = low_s.shape[1]

    bar = pltpu.get_barrier_semaphore()
    for j in range(1, 16):
        far = (col + j) % 16
        pl.semaphore_signal(bar, inc=1, device_id=((row + j) % 16, col), device_id_type=MESH)
        pl.semaphore_signal(bar, inc=1, device_id=(row, far), device_id_type=MESH)
        pl.semaphore_signal(bar, inc=1, device_id=(chip * 2 + 1 - core, far), device_id_type=MESH)

    loads = [
        pltpu.make_async_copy(src, dst, load_sem.at[n])
        for n, (src, dst) in enumerate(
            [
                (task, tsk_v), (task_emb, emb_v), (gen_in, gin_v), (count, cnt_v), (gen_a, ga_v),
                (tokens, tok_v), (gen_b, gb_v), (w_gate, wg_v), (w_up, wu_v), (w_down, wd_v),
            ]
        )
    ]
    for c in loads:
        c.start()

    def copy(src, dst, ss, rs, dev):
        return pltpu.make_async_remote_copy(
            src_ref=src, dst_ref=dst, send_sem=ss, recv_sem=rs, device_id=dev, device_id_type=MESH
        )

    gi = lax.broadcasted_iota(jnp.int32, (groups, groups), 0)
    gj = lax.broadcasted_iota(jnp.int32, (groups, groups), 1)
    loads[0].wait()
    task_of = jnp.sum(jnp.where(gi == gj, tsk_v[...].astype(F32), 0.0), axis=1, keepdims=True)
    tasks = emb_v.shape[0]
    pick = lax.broadcasted_iota(jnp.int32, (groups, tasks), 1).astype(F32) == task_of
    loads[1].wait()
    chosen = dot(jnp.where(pick, 1.0, 0.0).astype(BF16), emb_v[...]).astype(BF16)
    loads[2].wait()
    hyper = jax.nn.silu(dot(chosen, gin_v[...])).astype(BF16)

    loads[3].wait()
    cnt = cnt_v[...].astype(F32)
    ends = jnp.sum(jnp.where(gj <= gi, cnt, 0.0), axis=1, keepdims=True)
    starts = ends - jnp.sum(jnp.where(gj == gi, cnt, 0.0), axis=1, keepdims=True)

    def member(first, width):
        request = (lax.broadcasted_iota(jnp.int32, (groups, width), 1) + first) // 2
        request = request.astype(F32)
        return jnp.where((request >= starts) & (request < ends), 1.0, 0.0)

    loads[4].wait()
    fac_a = dot(ga_v[...], hyper, ((1,), (1,))).astype(BF16)
    n_tok = tok_v.shape[0]
    width = tok_v.shape[1]
    slab = fac_a.shape[0] // ranks
    a_of = dot(fac_a, member(0, n_tok).astype(BF16))
    which = lax.broadcasted_iota(jnp.int32, (slab * ranks, width), 0) // ranks + col * slab
    sel = jnp.where(lax.broadcasted_iota(jnp.int32, (slab * ranks, width), 1) == which, 1.0, 0.0)
    loads[5].wait()
    t_of = dot(sel.astype(BF16), tok_v[...], ((1,), (1,)))
    low = jnp.sum((a_of * t_of).reshape(slab, ranks, n_tok), axis=0)
    for h in range(2):
        for q in range(2):
            low_s[h, :, q, :] = low[:, h * 256 + q * 128 : h * 256 + q * 128 + 128]

    pl.semaphore_wait(bar, 45)

    l1 = []
    for j in range(1, 16):
        to = (row + j) % 16
        l1.append(
            copy(low_s.at[to % 2, pl.ds(to // 2 * 2, 2)], low1_r.at[j], l1_ss.at[j], l1_rs.at[j], (to, col))
        )
        l1[-1].start()
    mate = (chip * 2 + 1 - core, col)
    half = tok_v.shape[0] // 2
    other = pl.ds(pl.multiple_of((1 - core) * half, half), half)
    mine = pl.ds(pl.multiple_of(core * half, half), half)
    for n in (7, 8, 9):
        loads[n].wait()
    pair = [
        copy(tok_v.at[other], tokp_v, pair_ss.at[0], pair_rs.at[0], mate),
        copy(wg_v, wgp_v, pair_ss.at[1], pair_rs.at[1], mate),
        copy(wu_v, wup_v, pair_ss.at[2], pair_rs.at[2], mate),
        copy(wd_v, wdp_v, pair_ss.at[3], pair_rs.at[3], mate),
        copy(b_v.at[core], b_v.at[core], pair_ss.at[4], pair_rs.at[4], mate),
    ]
    for n in range(4):
        pair[n].start()
    loads[6].wait()
    b_v[core] = dot(hyper, gb_v[...]).astype(BF16)
    pair[4].start()

    gate = dot(tok_v[mine, :], wg_v[...])
    pair[0].wait_recv()
    pair[1].wait_recv()
    gate_s[...] = (gate + dot(tokp_v[...], wgp_v[...])).astype(BF16)
    share = half // 8

    def rows(i):
        return pl.ds(pl.multiple_of(i * share, share), share)

    def peer(j):
        return (chip + j) % 8

    gs = [
        copy(gate_s.at[rows(peer(j))], gate_r.at[j], g_ss.at[j], g_rs.at[j], (peer(j) * 2 + core, col))
        for j in range(1, 8)
    ]
    for c in gs:
        c.start()

    low1 = low_s[core, pl.ds(chip * 2, 2)]
    for j in range(1, 16):
        l1[j - 1].wait_recv()
        low1 = low1 + low1_r[j]
    low1_s[...] = low1
    l2 = []
    for j in range(1, 16):
        l2.append(copy(low1_s, low2_r.at[j], l2_ss.at[j], l2_rs.at[j], (row, (col + j) % 16)))
        l2[-1].start()

    up = dot(tok_v[mine, :], wu_v[...])
    pair[2].wait_recv()
    up = up + dot(tokp_v[...], wup_v[...])
    pair[4].wait_recv()
    for j in range(1, 16):
        l2[j - 1].wait_recv()
        low1 = low1 + low2_r[j]
    low1 = low1.astype(BF16).astype(F32)
    mem = member(core * half, half)
    spread = [
        (mem * jnp.concatenate([low1[a, 0:1, :], low1[a, 1:2, :]], axis=1)).astype(BF16) for a in range(2)
    ]
    b_all = b_v[...].reshape(2 * groups, b_v.shape[2])
    up = up + dot(jnp.concatenate(spread, axis=0), b_all, ((0,), (0,)))
    up_s[...] = up.astype(BF16)
    us = [
        copy(up_s.at[rows(peer(j))], up_r.at[j], u_ss.at[j], u_rs.at[j], (peer(j) * 2 + core, col))
        for j in range(1, 8)
    ]
    for c in us:
        c.start()

    gate_t = gate_s[rows(chip), :].astype(F32)
    for j in range(1, 8):
        gs[j - 1].wait_recv()
        gate_t = gate_t + gate_r[j].astype(F32)
    act = jax.nn.silu(gate_t)
    up_t = up_s[rows(chip), :].astype(F32)
    for j in range(1, 8):
        us[j - 1].wait_recv()
        up_t = up_t + up_r[j].astype(F32)
    hid_v[rows(chip), :] = (act * up_t).astype(BF16)

    hs = [
        copy(hid_v.at[rows(chip)], hid_v.at[rows(chip)], h_ss.at[j], h_rs.at[j], (peer(j) * 2 + core, col))
        for j in range(1, 8)
    ]
    for c in hs:
        c.start()
    pair[3].wait_recv()
    for j in range(1, 8):
        src = (chip + 8 - j) % 8
        copy(hid_v.at[rows(src)], hid_v.at[rows(src)], h_ss.at[j], h_rs.at[j], (row, col)).wait_recv()

    mix_own[...] = dot(hid_v[...], wd_v[...]).astype(BF16)
    mix_par[...] = dot(hid_v[...], wdp_v[...]).astype(BF16)
    own_half = col // 8 == core
    ms = []
    for j in range(8):
        b = (col + j) % 8
        to = core * 8 + b
        same = copy(mix_own.at[rows(b)], mix_r.at[col], m_ss.at[0, j], m_rs.at[col], (row, to))
        cross = copy(
            mix_par.at[rows(b)], mix_r.at[col], m_ss.at[1, j], m_rs.at[col], (chip * 2 + 1 - core, to)
        )
        ms.append((same, cross))
        if j == 0:
            pl.when(jnp.logical_not(own_half))(same.start)
        else:
            same.start()
        cross.start()

    @pl.when(own_half)
    def _():
        mix_r[col] = mix_own[rows(col % 8), :]

    for s in range(16):
        arrived = copy(mix_r.at[s], mix_r.at[s], m_ss.at[0, 0], m_rs.at[s], (row, col))
        pl.when(jnp.logical_not(own_half & (col == s)))(arrived.wait_recv)
    total = mix_r[0].astype(F32)
    for s in range(1, 16):
        total = total + mix_r[s].astype(F32)
    out[...] = total.astype(BF16)

    for c in l1 + l2 + pair + gs + us + hs:
        c.wait_send()
    for j in range(8):
        if j == 0:
            pl.when(jnp.logical_not(own_half))(ms[j][0].wait_send)
        else:
            ms[j][0].wait_send()
        ms[j][1].wait_send()


def shards(tokens, task_emb, gen_in, gen_a, gen_b, w_gate, w_up, w_down, group_count, group_task):
    batch, draft, width = tokens.shape
    hyper, slab, ranks = gen_a.shape
    groups = group_count.shape[0]
    units = w_gate.shape[1]
    n_tok = batch * draft
    half = n_tok // 2
    share = half // 8
    vm = pltpu.VMEM
    dma = pltpu.SemaphoreType.DMA
    args = (
        tokens.reshape(n_tok, width),
        task_emb,
        gen_in,
        gen_a.transpose(1, 2, 0).reshape(slab * ranks, hyper),
        gen_b.reshape(hyper, units),
        w_gate,
        w_up,
        w_down,
        group_count.reshape(1, groups),
        group_task.reshape(1, groups),
    )
    scratch = [vm(a.shape, a.dtype) for a in args]
    scratch += [
        vm((half, width), BF16),
        vm((width, units), BF16),
        vm((width, units), BF16),
        vm((units, width), BF16),
        vm((2, groups, units), BF16),
        vm((2, ranks, 2, half // 2), F32),
        vm((16, 2, 2, half // 2), F32),
        vm((2, 2, half // 2), F32),
        vm((16, 2, 2, half // 2), F32),
        vm((half, units), BF16),
        vm((half, units), BF16),
        vm((8, share, units), BF16),
        vm((8, share, units), BF16),
        vm((half, units), BF16),
        vm((half, width), BF16),
        vm((half, width), BF16),
        vm((16, share, width), BF16),
        dma((10,)), dma((5,)), dma((5,)), dma((16,)), dma((16,)), dma((16,)), dma((16,)),
        dma((8,)), dma((8,)), dma((8,)), dma((8,)), dma((8,)), dma((8,)), dma((2, 8)), dma((16,)),
    ]
    any_spec = pl.BlockSpec(memory_space=pl.ANY)
    out = pl.pallas_call(
        kernel,
        out_shape=jax.ShapeDtypeStruct((share, width), BF16),
        in_specs=[any_spec] * len(args),
        out_specs=pl.BlockSpec(memory_space=pltpu.VMEM),
        scratch_shapes=scratch,
        compiler_params=pltpu.CompilerParams(
            collective_id=0, has_side_effects=True, vmem_limit_bytes=56 * 1024 * 1024
        ),
    )(*args)
    return out.reshape(share // draft, draft, width)


def solution(mesh):
    placed = (
        P(None, None, "row"),
        P(),
        P(),
        P(None, ("row", "col"), None),
        P(None, "row", "col"),
        P("row", "col"),
        P("row", "col"),
        P("col", "row"),
        P(),
        P(),
    )
    return jax.shard_map(
        shards, mesh=mesh, in_specs=placed, out_specs=P("col", None, "row"), check_vma=False
    )
```

time: 138 us -> 53 us (0.38)
  the two profiles are of different devices: /device:TPU:32 before, /device:TPU:1 now
where the time goes in v1:
time: 53 us; the launch traced here: 52.9 us
  Pallas kernels  49.8 us (94%)
  local copies, waits for them, and re-layouts  3.08 us (6%)
    pallas_call x1, Pallas kernels, shards(): pl.pallas_call(kernel, out_shape=jax.ShapeDtypeStruct((share, width), BF1...  49.8 us
    reshape x1, local copies, waits for them, and re-layouts, shards(): tokens.reshape(n_tok, width)  1.74 us
    reshape x1, local copies, waits for them, and re-layouts, shards(): return out.reshape(share // draft, draft, width)  1.34 us

profile of v1, /device:TPU:1, one launch (start us, length us, event | category | flops | bytes accessed | tf_op | source)
XLA Modules:
  0.0 52.9 jit_solution(14014340254473496410)
XLA Ops:
  0.0 1.7 %reshape.18.tokens = bf16[512,256]{1,0:T(8,128)(2,1)} reshape(bf16[256,2,256]{2,1,0:T(2,128)(2,1)} %param.10) | data formatting | bytes 524288 | tf_op jit(solution)/shard_map/reshape | solution.py:248
  1.7 49.8 %shard_map.100 = bf16[32,256]{1,0:T(8,128)(2,1)} custom-call(bf16[512,256]{1,0:T(8,128)(2,1)} %reshape.18.tokens, bf16[512,1024]{1,0:T(8,128)(2,1)} %task_emb.1, bf16[1024,512]{1,0:T(8,128)(2,1)} %gen_in.1, bf16[256,512]{1,0:T(8,128)(2,1)} %bitcast.7, bf16[512,896]{1,0:T(8,128)(2,1)} %bitcast.6, bf16[256,896]{1,0:T(8,128)(2,1)} %w_gate.1, ...), custom_call_target="tpu_custom_call" | custom-call | tf_op jit(solution)/shard_map/pallas_call | solution.py:282
  51.5 1.3 %reshape.23 = bf16[16,2,256]{2,1,0:T(2,128)(2,1)} reshape(bf16[32,256]{1,0:T(8,128)(2,1)} %shard_map.100) | data formatting | bytes 32768 | tf_op jit(solution)/shard_map/reshape | solution.py:292

commit v2 on v1

v2 whole, which is shorter than its diff:
```python
import functools

import jax
import jax.numpy as jnp
from jax import lax
from jax.experimental import pallas as pl
from jax.experimental.pallas import tpu as pltpu
from jax.sharding import PartitionSpec as P

MESH = pl.DeviceIdType.MESH
F32 = jnp.float32
BF16 = jnp.bfloat16


def dot(a, b, dims=((1,), (0,))):
    return lax.dot_general(a, b, (dims, ((), ())), preferred_element_type=F32)


def kernel(
    tokens, task_emb, gen_in, gen_a, gen_b, w_gate, w_up, w_down, count, task,
    out,
    tok3_v, emb_v, gin_v, ga_v, gb_v, wg_v, wu_v, wd_v, cnt_v, tsk_v,
    tok_v, tokp_v, wgp_v, wup_v, wdp_v, b_v,
    low_s, low1_r, lowx_s, lowx_r, lowz_s, lowz_r,
    gate_s, up_s, gate_r, up_r, hid_v, mix_s, mix_r,
    load_sem, pair_ss, pair_rs, l1_ss, l1_rs, lx_ss, lx_rs, lz_ss, lz_rs,
    g_ss, g_rs, u_ss, u_rs, h_ss, h_rs, m_ss, m_rs,
):
    row = lax.axis_index("row")
    col = lax.axis_index("col")
    z_lo, y, core = row // 8, row // 2 % 4, row % 2
    z_hi, x = col // 4, col % 4
    chip = row // 2
    groups = count.shape[1]
    ranks = low_s.shape[1]
    mate = (row + 1 - 2 * core, col)

    def in_row(dz, dy, dk, sign=1):
        return ((z_lo + dz) % 2 * 4 + (y + sign * dy + 4) % 4) * 2 + (core + dk) % 2

    def in_col(dz, dx):
        return (z_hi + dz) % 4 * 4 + (x + dx) % 4

    row_steps = [(dz, dy, dk) for dz in (1, 0) for dy in (2, 1, 3, 0) for dk in (1, 0)][:-1]
    chip_steps = [(dz, dy) for dz in (1, 0) for dy in (2, 1, 3, 0)][:-1]

    bar = pltpu.get_barrier_semaphore()
    for d in (2, 1, 3):
        pl.semaphore_signal(bar, inc=1, device_id=(row, in_col(d, 0)), device_id_type=MESH)
    for step in row_steps:
        pl.semaphore_signal(bar, inc=1, device_id=(in_row(*step), col), device_id_type=MESH)
    for d in (2, 1, 3):
        pl.semaphore_signal(bar, inc=1, device_id=(row, in_col(0, d)), device_id_type=MESH)

    loads = [
        pltpu.make_async_copy(src, dst, load_sem.at[n])
        for n, (src, dst) in enumerate(
            [
                (task, tsk_v), (task_emb, emb_v), (gen_in, gin_v), (count, cnt_v), (gen_a, ga_v),
                (tokens, tok3_v), (gen_b, gb_v), (w_gate, wg_v), (w_up, wu_v), (w_down, wd_v),
            ]
        )
    ]
    for c in loads:
        c.start()

    def copy(src, dst, ss, rs, dev):
        return pltpu.make_async_remote_copy(
            src_ref=src, dst_ref=dst, send_sem=ss, recv_sem=rs, device_id=dev, device_id_type=MESH
        )

    gi = lax.broadcasted_iota(jnp.int32, (groups, groups), 0)
    gj = lax.broadcasted_iota(jnp.int32, (groups, groups), 1)
    loads[0].wait()
    task_of = jnp.sum(jnp.where(gi == gj, tsk_v[...].astype(F32), 0.0), axis=1, keepdims=True)
    tasks = emb_v.shape[0]
    pick = lax.broadcasted_iota(jnp.int32, (groups, tasks), 1).astype(F32) == task_of
    loads[1].wait()
    chosen = dot(jnp.where(pick, 1.0, 0.0).astype(BF16), emb_v[...]).astype(BF16)
    loads[2].wait()
    hyper = jax.nn.silu(dot(chosen, gin_v[...])).astype(BF16)

    loads[3].wait()
    cnt = cnt_v[...].astype(F32)
    ends = jnp.sum(jnp.where(gj <= gi, cnt, 0.0), axis=1, keepdims=True)
    starts = ends - jnp.sum(jnp.where(gj == gi, cnt, 0.0), axis=1, keepdims=True)

    def member(first, width):
        request = (lax.broadcasted_iota(jnp.int32, (groups, width), 1) + first) // 2
        request = request.astype(F32)
        return jnp.where((request >= starts) & (request < ends), 1.0, 0.0)

    loads[4].wait()
    fac_a = dot(ga_v[...], hyper, ((1,), (1,))).astype(BF16)
    n_tok = tok_v.shape[0]
    width = tok_v.shape[1]
    slab = fac_a.shape[0] // ranks
    a_of = dot(fac_a, member(0, n_tok).astype(BF16))
    which = lax.broadcasted_iota(jnp.int32, (slab * ranks, width), 0) // ranks + col * slab
    sel = jnp.where(lax.broadcasted_iota(jnp.int32, (slab * ranks, width), 1) == which, 1.0, 0.0)
    loads[5].wait()
    tok_v[...] = tok3_v[...].reshape(n_tok, width)
    t_of = dot(sel.astype(BF16), tok_v[...], ((1,), (1,)))
    low = jnp.sum((a_of * t_of).reshape(slab, ranks, n_tok), axis=0)
    for h in range(2):
        for q in range(2):
            low_s[h, :, q, :] = low[:, h * 256 + q * 128 : h * 256 + q * 128 + 128]

    pl.semaphore_wait(bar, 21)

    l1 = []
    for n, (dz, dy, dk) in enumerate(row_steps):
        to = in_row(dz, dy, dk)
        l1.append(
            copy(low_s.at[to % 2, pl.ds(to // 2 * 2, 2)], low1_r.at[n], l1_ss.at[n], l1_rs.at[n], (to, col))
        )
        l1[-1].start()
    half = tok_v.shape[0] // 2
    other = pl.ds(pl.multiple_of((1 - core) * half, half), half)
    mine = pl.ds(pl.multiple_of(core * half, half), half)
    for n in (7, 8, 9):
        loads[n].wait()
    pair = [
        copy(tok_v.at[other], tokp_v, pair_ss.at[0], pair_rs.at[0], mate),
        copy(wg_v, wgp_v, pair_ss.at[1], pair_rs.at[1], mate),
        copy(wu_v, wup_v, pair_ss.at[2], pair_rs.at[2], mate),
        copy(wd_v, wdp_v, pair_ss.at[3], pair_rs.at[3], mate),
        copy(b_v.at[core], b_v.at[core], pair_ss.at[4], pair_rs.at[4], mate),
    ]
    for n in range(4):
        pair[n].start()
    loads[6].wait()
    b_v[core] = dot(hyper, gb_v[...]).astype(BF16)
    pair[4].start()

    gate = dot(tok_v[mine, :], wg_v[...])
    pair[0].wait_recv()
    pair[1].wait_recv()
    gate_s[...] = (gate + dot(tokp_v[...], wgp_v[...])).astype(BF16)
    share = half // 8
    part = share // 2

    def rows(i, first=0, size=share):
        return pl.ds(pl.multiple_of(i * share + first, size), size)

    def peer(dz, dy, sign=1):
        return in_row(dz, dy, 0, sign) // 2

    gs = []
    for n, (dz, dy) in enumerate(chip_steps):
        i = peer(dz, dy)
        gs.append(copy(gate_s.at[rows(i)], gate_r.at[n], g_ss.at[n], g_rs.at[n], (i * 2 + core, col)))
    for n, (dz, dy) in enumerate(chip_steps):
        if dz == 0:
            gs[n].start()

    low1 = low_s[core, pl.ds(chip * 2, 2)]
    for n in range(15):
        l1[n].wait_recv()
        low1 = low1 + low1_r[n]
    lowx_s[...] = low1
    lx = [
        copy(lowx_s, lowx_r.at[n], lx_ss.at[n], lx_rs.at[n], (row, in_col(0, d)))
        for n, d in enumerate((2, 1, 3))
    ]
    for c in lx:
        c.start()
    up = dot(tok_v[mine, :], wu_v[...])
    for n in range(3):
        lx[n].wait_recv()
        low1 = low1 + lowx_r[n]
    lowz_s[...] = low1
    lz = [
        copy(lowz_s, lowz_r.at[n], lz_ss.at[n], lz_rs.at[n], (row, in_col(d, 0)))
        for n, d in enumerate((2, 1, 3))
    ]
    for c in lz:
        c.start()
    for n, (dz, dy) in enumerate(chip_steps):
        if dz == 1:
            gs[n].start()

    pair[2].wait_recv()
    up = up + dot(tokp_v[...], wup_v[...])
    pair[4].wait_recv()
    mem = member(core * half, half)
    b_all = b_v[...].reshape(2 * groups, b_v.shape[2])
    for n in range(3):
        lz[n].wait_recv()
        low1 = low1 + lowz_r[n]
    low1 = low1.astype(BF16).astype(F32)
    spread = [
        (mem * jnp.concatenate([low1[a, 0:1, :], low1[a, 1:2, :]], axis=1)).astype(BF16) for a in range(2)
    ]
    up = up + dot(jnp.concatenate(spread, axis=0), b_all, ((0,), (0,)))
    up_s[...] = up.astype(BF16)
    us = []
    for a in range(2):
        us.append([])
        for n, (dz, dy) in enumerate(chip_steps):
            i = peer(dz, dy)
            us[a].append(
                copy(
                    up_s.at[rows(i, a * part, part)], up_r.at[a, n], u_ss.at[a, n], u_rs.at[a, n],
                    (i * 2 + core, col),
                )
            )
            us[a][-1].start()

    gate_t = gate_s[rows(chip), :].astype(F32)
    for n in range(7):
        gs[n].wait_recv()
        gate_t = gate_t + gate_r[n].astype(F32)
    act = jax.nn.silu(gate_t)
    hs = []
    for a in range(2):
        up_t = up_s[rows(chip, a * part, part), :].astype(F32)
        for n in range(7):
            us[a][n].wait_recv()
            up_t = up_t + up_r[a, n].astype(F32)
        hid_v[a, chip] = (act[a * part : a * part + part] * up_t).astype(BF16)
        hs.append([])
        for n, (dz, dy) in enumerate(chip_steps):
            hs[a].append(
                copy(
                    hid_v.at[a, chip], hid_v.at[a, chip], h_ss.at[a, n], h_rs.at[a, n],
                    (peer(dz, dy) * 2 + core, col),
                )
            )
            hs[a][-1].start()

    pair[3].wait_recv()
    own_half = col // 8 == core
    d = (z_hi - 2 * core + 4) % 4
    far = 1 - (d + 1) // 2 % 2
    ms = []
    for a in range(2):
        for n, (dz, dy) in enumerate(chip_steps):
            src = peer(dz, dy, -1)
            copy(hid_v.at[a, src], hid_v.at[a, src], h_ss.at[a, n], h_rs.at[a, n], (row, col)).wait_recv()
        hid = hid_v[a].reshape(8 * part, hid_v.shape[3])
        mix_s[a, 0] = dot(hid, wd_v[...]).astype(BF16).reshape(8, part, width)
        mix_s[a, 1] = dot(hid, wdp_v[...]).astype(BF16).reshape(8, part, width)
        for t in range(2):
            for n, dx in enumerate((2, 1, 3, 0)):
                b = (far + t) % 2 * 4 + (x + dx) % 4
                to = core * 8 + b
                cross = copy(
                    mix_s.at[a, 1, b], mix_r.at[a, col], m_ss.at[a, t, n, 1], m_rs.at[a, col], (mate[0], to)
                )
                cross.start()
                same = copy(
                    mix_s.at[a, 0, b], mix_r.at[a, col], m_ss.at[a, t, n, 0], m_rs.at[a, col], (row, to)
                )
                local = t == 1 and dx == 0
                if local:
                    pl.when(jnp.logical_not(own_half))(same.start)
                else:
                    same.start()
                ms.append((cross, same, local))

        @pl.when(own_half)
        def _():
            mix_r[a, col] = mix_s[a, 0, col % 8]

    for a in range(2):
        for s in range(16):
            arrived = copy(mix_r.at[a, s], mix_r.at[a, s], m_ss.at[a, 0, 0, 0], m_rs.at[a, s], (row, col))
            pl.when(jnp.logical_not(own_half & (col == s)))(arrived.wait_recv)
        total = mix_r[a, 0].astype(F32)
        for s in range(1, 16):
            total = total + mix_r[a, s].astype(F32)
        out[pl.ds(a * part, part), :] = total.astype(BF16)

    for c in l1 + lx + lz + pair + gs + us[0] + us[1] + hs[0] + hs[1]:
        c.wait_send()
    for cross, same, local in ms:
        cross.wait_send()
        if local:
            pl.when(jnp.logical_not(own_half))(same.wait_send)
        else:
            same.wait_send()


def shards(tokens, task_emb, gen_in, gen_a, gen_b, w_gate, w_up, w_down, group_count, group_task):
    batch, draft, width = tokens.shape
    hyper, slab, ranks = gen_a.shape
    groups = group_count.shape[0]
    units = w_gate.shape[1]
    n_tok = batch * draft
    half = n_tok // 2
    share = half // 8
    part = share // 2
    vm = pltpu.VMEM
    dma = pltpu.SemaphoreType.DMA
    args = (
        tokens,
        task_emb,
        gen_in,
        gen_a.transpose(1, 2, 0).reshape(slab * ranks, hyper),
        gen_b.reshape(hyper, units),
        w_gate,
        w_up,
        w_down,
        group_count.reshape(1, groups),
        group_task.reshape(1, groups),
    )
    scratch = [vm(a.shape, a.dtype) for a in args]
    scratch += [
        vm((n_tok, width), BF16),
        vm((half, width), BF16),
        vm((width, units), BF16),
        vm((width, units), BF16),
        vm((units, width), BF16),
        vm((2, groups, units), BF16),
        vm((2, ranks, 2, half // 2), F32),
        vm((15, 2, 2, half // 2), F32),
        vm((2, 2, half // 2), F32),
        vm((3, 2, 2, half // 2), F32),
        vm((2, 2, half // 2), F32),
        vm((3, 2, 2, half // 2), F32),
        vm((half, units), BF16),
        vm((half, units), BF16),
        vm((7, share, units), BF16),
        vm((2, 7, part, units), BF16),
        vm((2, 8, part, units), BF16),
        vm((2, 2, 8, part, width), BF16),
        vm((2, 16, part, width), BF16),
    ]
    scratch += [
        dma(n)
        for n in (
            (10,), (5,), (5,), (15,), (15,), (3,), (3,), (3,), (3,),
            (7,), (7,), (2, 7), (2, 7), (2, 7), (2, 7), (2, 2, 4, 2), (2, 16),
        )
    ]
    any_spec = pl.BlockSpec(memory_space=pl.ANY)
    out = pl.pallas_call(
        kernel,
        out_shape=jax.ShapeDtypeStruct((share, width), BF16),
        in_specs=[any_spec] * len(args),
        out_specs=pl.BlockSpec(memory_space=pltpu.VMEM),
        scratch_shapes=scratch,
        compiler_params=pltpu.CompilerParams(
            collective_id=0, has_side_effects=True, vmem_limit_bytes=56 * 1024 * 1024
        ),
    )(*args)
    return out.reshape(share // draft, draft, width)


def solution(mesh):
    placed = (
        P(None, None, "row"),
        P(),
        P(),
        P(None, ("row", "col"), None),
        P(None, "row", "col"),
        P("row", "col"),
        P("row", "col"),
        P("col", "row"),
        P(),
        P(),
    )
    return jax.shard_map(
        shards, mesh=mesh, in_specs=placed, out_specs=P("col", None, "row"), check_vma=False
    )
```

time: 53 us -> 47.4 us (0.89)
  Pallas kernels: 49.8 us -> 45.9 us
  local copies, waits for them, and re-layouts: 3.08 us -> 1.34 us
    pallas_call x1, Pallas kernels: 49.8 us -> 45.9 us  [shards(): pl.pallas_call(kernel, out_shape=jax.ShapeDtypeStruct((share, width), BF1...]
    reshape x1 -> x0, local copies, waits for them, and re-layouts: 1.74 us -> none  [shards(): tokens.reshape(n_tok, width)]
where the time goes in v2:
time: 47.4 us; the launch traced here: 47.2 us
  Pallas kernels  45.9 us (97%)
  local copies, waits for them, and re-layouts  1.34 us (3%)
    pallas_call x1, Pallas kernels, shards(): pl.pallas_call(kernel, out_shape=jax.ShapeDtypeStruct((share, width), BF1...  45.9 us
    reshape x1, local copies, waits for them, and re-layouts, shards(): return out.reshape(share // draft, draft, width)  1.34 us

profile of v2, /device:TPU:1, one launch (start us, length us, event | category | flops | bytes accessed | tf_op | source)
XLA Modules:
  0.0 47.2 jit_solution(194638682243115287)
XLA Ops:
  0.0 45.9 %shard_map.100 = bf16[32,256]{1,0:T(8,128)(2,1)} custom-call(bf16[256,2,256]{2,1,0:T(2,128)(2,1)} %tokens.1, bf16[512,1024]{1,0:T(8,128)(2,1)} %task_emb.1, bf16[1024,512]{1,0:T(8,128)(2,1)} %gen_in.1, bf16[256,512]{1,0:T(8,128)(2,1)} %bitcast.7, bf16[512,896]{1,0:T(8,128)(2,1)} %bitcast.6, bf16[256,896]{1,0:T(8,128)(2,1)} %w_gate.1, bf16[256,896]{1,0:T(8,128)(2,1)} %w_up.1, ...), custom_call_target="tpu_custom_call" | custom-call | tf_op jit(solution)/shard_map/pallas_call | solution.py:338
  45.9 1.3 %reshape.19 = bf16[16,2,256]{2,1,0:T(2,128)(2,1)} reshape(bf16[32,256]{1,0:T(8,128)(2,1)} %shard_map.100) | data formatting | bytes 32768 | tf_op jit(solution)/shard_map/reshape | solution.py:348

commit v3 on v2

--- a/solution.py
+++ b/solution.py
@@ -21,10 +21,10 @@
     out,
     tok3_v, emb_v, gin_v, ga_v, gb_v, wg_v, wu_v, wd_v, cnt_v, tsk_v,
     tok_v, tokp_v, wgp_v, wup_v, wdp_v, b_v,
-    low_s, low1_r, lowx_s, lowx_r, lowz_s, lowz_r,
-    gate_s, up_s, gate_r, up_r, hid_v, mix_s, mix_r,
-    load_sem, pair_ss, pair_rs, l1_ss, l1_rs, lx_ss, lx_rs, lz_ss, lz_rs,
-    g_ss, g_rs, u_ss, u_rs, h_ss, h_rs, m_ss, m_rs,
+    low_s, low1_r, low2_s, low2_r,
+    gate_s, up_f, up_s, gate_r, up_r, hid_v, mix_f, mix_s, mix_r, end_s, end_r,
+    known, load_sem, pair_ss, pair_rs, l1_ss, l1_rs, l2_ss, l2_rs,
+    g_ss, g_rs, u_ss, u_rs, h_ss, h_rs, m_ss, m_rs, e_ss, e_rs,
 ):
     row = lax.axis_index("row")
     col = lax.axis_index("col")
@@ -42,6 +42,7 @@
         return (z_hi + dz) % 4 * 4 + (x + dx) % 4
 
     row_steps = [(dz, dy, dk) for dz in (1, 0) for dy in (2, 1, 3, 0) for dk in (1, 0)][:-1]
+    col_steps = [(dz, dx) for dz in (2, 1, 3, 0) for dx in (2, 1, 3, 0)][:-1]
     chip_steps = [(dz, dy) for dz in (1, 0) for dy in (2, 1, 3, 0)][:-1]
 
     bar = pltpu.get_barrier_semaphore()
@@ -107,6 +108,8 @@
             low_s[h, :, q, :] = low[:, h * 256 + q * 128 : h * 256 + q * 128 + 128]
 
     pl.semaphore_wait(bar, 21)
+    for d in (2, 1, 3):
+        pl.semaphore_signal(known, inc=1, device_id=(row, in_col(d, 0)), device_id_type=MESH)
 
     l1 = []
     for n, (dz, dy, dk) in enumerate(row_steps):
@@ -136,12 +139,10 @@
     gate = dot(tok_v[mine, :], wg_v[...])
     pair[0].wait_recv()
     pair[1].wait_recv()
-    gate_s[...] = (gate + dot(tokp_v[...], wgp_v[...])).astype(BF16)
     share = half // 8
     part = share // 2
-
-    def rows(i, first=0, size=share):
-        return pl.ds(pl.multiple_of(i * share + first, size), size)
+    units = gate.shape[1]
+    gate_s[...] = (gate + dot(tokp_v[...], wgp_v[...])).astype(BF16).reshape(2, 8, part, units)
 
     def peer(dz, dy, sign=1):
         return in_row(dz, dy, 0, sign) // 2
@@ -149,76 +150,62 @@
     gs = []
     for n, (dz, dy) in enumerate(chip_steps):
         i = peer(dz, dy)
-        gs.append(copy(gate_s.at[rows(i)], gate_r.at[n], g_ss.at[n], g_rs.at[n], (i * 2 + core, col)))
+        gs.append(copy(gate_s.at[:, i], gate_r.at[n], g_ss.at[n], g_rs.at[n], (i * 2 + core, col)))
     for n, (dz, dy) in enumerate(chip_steps):
         if dz == 0:
             gs[n].start()
 
-    low1 = low_s[core, pl.ds(chip * 2, 2)]
+    low = low_s[core, pl.ds(chip * 2, 2)]
     for n in range(15):
         l1[n].wait_recv()
-        low1 = low1 + low1_r[n]
-    lowx_s[...] = low1
-    lx = [
-        copy(lowx_s, lowx_r.at[n], lx_ss.at[n], lx_rs.at[n], (row, in_col(0, d)))
-        for n, d in enumerate((2, 1, 3))
-    ]
-    for c in lx:
-        c.start()
-    up = dot(tok_v[mine, :], wu_v[...])
-    for n in range(3):
-        lx[n].wait_recv()
-        low1 = low1 + lowx_r[n]
-    lowz_s[...] = low1
-    lz = [
-        copy(lowz_s, lowz_r.at[n], lz_ss.at[n], lz_rs.at[n], (row, in_col(d, 0)))
-        for n, d in enumerate((2, 1, 3))
-    ]
-    for c in lz:
-        c.start()
+        low = low + low1_r[n]
+    low2_s[...] = low
+    pl.semaphore_wait(known, 3)
+    l2 = []
+    for n, (dz, dx) in enumerate(col_steps):
+        l2.append(copy(low2_s, low2_r.at[n], l2_ss.at[n], l2_rs.at[n], (row, in_col(dz, dx))))
+        l2[-1].start()
     for n, (dz, dy) in enumerate(chip_steps):
         if dz == 1:
             gs[n].start()
 
+    up = dot(tok_v[mine, :], wu_v[...])
     pair[2].wait_recv()
-    up = up + dot(tokp_v[...], wup_v[...])
+    up_f[...] = up + dot(tokp_v[...], wup_v[...])
     pair[4].wait_recv()
-    mem = member(core * half, half)
-    b_all = b_v[...].reshape(2 * groups, b_v.shape[2])
-    for n in range(3):
-        lz[n].wait_recv()
-        low1 = low1 + lowz_r[n]
-    low1 = low1.astype(BF16).astype(F32)
-    spread = [
-        (mem * jnp.concatenate([low1[a, 0:1, :], low1[a, 1:2, :]], axis=1)).astype(BF16) for a in range(2)
-    ]
-    up = up + dot(jnp.concatenate(spread, axis=0), b_all, ((0,), (0,)))
-    up_s[...] = up.astype(BF16)
+    b_all = b_v[...].reshape(2 * groups, units)
+    block = half // 2
+    mem = [member(core * half + a * block, block) for a in range(2)]
+    for n in range(15):
+        l2[n].wait_recv()
+        low = low + low2_r[n]
+    low = low.astype(BF16).astype(F32)
     us = []
     for a in range(2):
+        spread = jnp.concatenate([mem[a] * low[r, a : a + 1, :] for r in range(2)], axis=0).astype(BF16)
+        up = up_f[a * block : a * block + block, :] + dot(spread, b_all, ((0,), (0,)))
+        up_s[a] = up.astype(BF16).reshape(8, part, units)
         us.append([])
         for n, (dz, dy) in enumerate(chip_steps):
             i = peer(dz, dy)
             us[a].append(
-                copy(
-                    up_s.at[rows(i, a * part, part)], up_r.at[a, n], u_ss.at[a, n], u_rs.at[a, n],
-                    (i * 2 + core, col),
-                )
+                copy(up_s.at[a, i], up_r.at[a, n], u_ss.at[a, n], u_rs.at[a, n], (i * 2 + core, col))
             )
             us[a][-1].start()
 
-    gate_t = gate_s[rows(chip), :].astype(F32)
     for n in range(7):
         gs[n].wait_recv()
-        gate_t = gate_t + gate_r[n].astype(F32)
-    act = jax.nn.silu(gate_t)
     hs = []
     for a in range(2):
-        up_t = up_s[rows(chip, a * part, part), :].astype(F32)
+        gate = gate_s[a, chip].astype(F32)
+        for n in range(7):
+            gate = gate + gate_r[n, a].astype(F32)
+        act = jax.nn.silu(gate)
+        up = up_s[a, chip].astype(F32)
         for n in range(7):
             us[a][n].wait_recv()
-            up_t = up_t + up_r[a, n].astype(F32)
-        hid_v[a, chip] = (act[a * part : a * part + part] * up_t).astype(BF16)
+            up = up + up_r[a, n].astype(F32)
+        hid_v[a, chip] = (act * up).astype(BF16)
         hs.append([])
         for n, (dz, dy) in enumerate(chip_steps):
             hs[a].append(
@@ -230,56 +217,56 @@
             hs[a][-1].start()
 
     pair[3].wait_recv()
-    own_half = col // 8 == core
-    d = (z_hi - 2 * core + 4) % 4
-    far = 1 - (d + 1) // 2 % 2
     ms = []
     for a in range(2):
         for n, (dz, dy) in enumerate(chip_steps):
             src = peer(dz, dy, -1)
             copy(hid_v.at[a, src], hid_v.at[a, src], h_ss.at[a, n], h_rs.at[a, n], (row, col)).wait_recv()
-        hid = hid_v[a].reshape(8 * part, hid_v.shape[3])
-        mix_s[a, 0] = dot(hid, wd_v[...]).astype(BF16).reshape(8, part, width)
-        mix_s[a, 1] = dot(hid, wdp_v[...]).astype(BF16).reshape(8, part, width)
-        for t in range(2):
-            for n, dx in enumerate((2, 1, 3, 0)):
-                b = (far + t) % 2 * 4 + (x + dx) % 4
-                to = core * 8 + b
-                cross = copy(
-                    mix_s.at[a, 1, b], mix_r.at[a, col], m_ss.at[a, t, n, 1], m_rs.at[a, col], (mate[0], to)
-                )
-                cross.start()
-                same = copy(
-                    mix_s.at[a, 0, b], mix_r.at[a, col], m_ss.at[a, t, n, 0], m_rs.at[a, col], (row, to)
-                )
-                local = t == 1 and dx == 0
-                if local:
-                    pl.when(jnp.logical_not(own_half))(same.start)
-                else:
-                    same.start()
-                ms.append((cross, same, local))
-
-        @pl.when(own_half)
+        hid = hid_v[a].reshape(block, units)
+        for k, w in enumerate((wd_v, wdp_v)):
+            mix = dot(hid, w[...])
+            mix_f[a, k] = mix.reshape(4, share, width)
+            mix_s[a, k] = mix.astype(BF16).reshape(4, share, width)
+        ms.append([])
+        for n, d in enumerate((2, 1, 3)):
+            ms[a].append(
+                copy(mix_s.at[a, :, (x + d) % 4], mix_r.at[a, n], m_ss.at[a, n], m_rs.at[a, n], (row, in_col(0, d)))
+            )
+            ms[a][-1].start()
+    es = []
+    for a in range(2):
+        to = 2 * core + a
+        here = z_hi == to
+        mix = mix_f[a, :, x]
+        for n in range(3):
+            ms[a][n].wait_recv()
+            mix = mix + mix_r[a, n].astype(F32)
+        end_s[a] = mix.astype(BF16)
+        cross = copy(end_s.at[a, 1], end_r.at[z_hi], e_ss.at[a, 1], e_rs.at[z_hi], (mate[0], to * 4 + x))
+        same = copy(end_s.at[a, 0], end_r.at[z_hi], e_ss.at[a, 0], e_rs.at[z_hi], (row, to * 4 + x))
+        pl.when(jnp.logical_not(here))(same.start)
+        cross.start()
+
+        @pl.when(here)
         def _():
-            mix_r[a, col] = mix_s[a, 0, col % 8]
-
-    for a in range(2):
-        for s in range(16):
-            arrived = copy(mix_r.at[a, s], mix_r.at[a, s], m_ss.at[a, 0, 0, 0], m_rs.at[a, s], (row, col))
-            pl.when(jnp.logical_not(own_half & (col == s)))(arrived.wait_recv)
-        total = mix_r[a, 0].astype(F32)
-        for s in range(1, 16):
-            total = total + mix_r[a, s].astype(F32)
-        out[pl.ds(a * part, part), :] = total.astype(BF16)
-
-    for c in l1 + lx + lz + pair + gs + us[0] + us[1] + hs[0] + hs[1]:
+            end_r[z_hi] = end_s[a, 0]
+
+        es.append((same, cross, here))
+
+    mine = z_hi // 2 == core
+    for s in range(4):
+        arrived = copy(end_r.at[s], end_r.at[s], e_ss.at[0, 0], e_rs.at[s], (row, col))
+        pl.when(jnp.logical_not(mine & (z_hi == s)))(arrived.wait_recv)
+    total = end_r[0].astype(F32)
+    for s in range(1, 4):
+        total = total + end_r[s].astype(F32)
+    out[...] = total.astype(BF16)
+
+    for c in l1 + l2 + pair + gs + us[0] + us[1] + hs[0] + hs[1] + ms[0] + ms[1]:
         c.wait_send()
-    for cross, same, local in ms:
+    for same, cross, here in es:
+        pl.when(jnp.logical_not(here))(same.wait_send)
         cross.wait_send()
-        if local:
-            pl.when(jnp.logical_not(own_half))(same.wait_send)
-        else:
-            same.wait_send()
 
 
 def shards(tokens, task_emb, gen_in, gen_a, gen_b, w_gate, w_up, w_down, group_count, group_task):
@@ -316,22 +303,25 @@
         vm((2, ranks, 2, half // 2), F32),
         vm((15, 2, 2, half // 2), F32),
         vm((2, 2, half // 2), F32),
-        vm((3, 2, 2, half // 2), F32),
-        vm((2, 2, half // 2), F32),
-        vm((3, 2, 2, half // 2), F32),
-        vm((half, units), BF16),
-        vm((half, units), BF16),
-        vm((7, share, units), BF16),
+        vm((15, 2, 2, half // 2), F32),
+        vm((2, 8, part, units), BF16),
+        vm((half, units), F32),
+        vm((2, 8, part, units), BF16),
+        vm((7, 2, part, units), BF16),
         vm((2, 7, part, units), BF16),
         vm((2, 8, part, units), BF16),
-        vm((2, 2, 8, part, width), BF16),
-        vm((2, 16, part, width), BF16),
+        vm((2, 2, 4, share, width), F32),
+        vm((2, 2, 4, share, width), BF16),
+        vm((2, 3, 2, share, width), BF16),
+        vm((2, 2, share, width), BF16),
+        vm((4, share, width), BF16),
+        pltpu.SemaphoreType.REGULAR,
     ]
     scratch += [
         dma(n)
         for n in (
-            (10,), (5,), (5,), (15,), (15,), (3,), (3,), (3,), (3,),
-            (7,), (7,), (2, 7), (2, 7), (2, 7), (2, 7), (2, 2, 4, 2), (2, 16),
+            (10,), (5,), (5,), (15,), (15,), (15,), (15,),
+            (7,), (7,), (2, 7), (2, 7), (2, 7), (2, 7), (2, 3), (2, 3), (2, 2), (4,),
         )
     ]
     any_spec = pl.BlockSpec(memory_space=pl.ANY)

time: 47.4 us -> 43.8 us (0.924)
  Pallas kernels: 45.9 us -> 42.3 us
    pallas_call x1, Pallas kernels: 45.9 us -> 42.3 us  [shards(): pl.pallas_call(kernel, out_shape=jax.ShapeDtypeStruct((share, width), BF1...]
where the time goes in v3:
time: 43.8 us; the launch traced here: 43.6 us
  Pallas kernels  42.3 us (97%)
  local copies, waits for them, and re-layouts  1.34 us (3%)
    pallas_call x1, Pallas kernels, shards(): pl.pallas_call(kernel, out_shape=jax.ShapeDtypeStruct((share, width), BF1...  42.3 us
    reshape x1, local copies, waits for them, and re-layouts, shards(): return out.reshape(share // draft, draft, width)  1.34 us

profile of v3, /device:TPU:1, one launch (start us, length us, event | category | flops | bytes accessed | tf_op | source)
XLA Modules:
  0.0 43.6 jit_solution(11944044634850486666)
XLA Ops:
  0.0 42.3 %shard_map.100 = bf16[32,256]{1,0:T(8,128)(2,1)} custom-call(bf16[256,2,256]{2,1,0:T(2,128)(2,1)} %tokens.1, bf16[512,1024]{1,0:T(8,128)(2,1)} %task_emb.1, bf16[1024,512]{1,0:T(8,128)(2,1)} %gen_in.1, bf16[256,512]{1,0:T(8,128)(2,1)} %bitcast.7, bf16[512,896]{1,0:T(8,128)(2,1)} %bitcast.6, bf16[256,896]{1,0:T(8,128)(2,1)} %w_gate.1, bf16[256,896]{1,0:T(8,128)(2,1)} %w_up.1, ...), custom_call_target="tpu_custom_call" | custom-call | tf_op jit(solution)/shard_map/pallas_call | solution.py:328
  42.3 1.3 %reshape.19 = bf16[16,2,256]{2,1,0:T(2,128)(2,1)} reshape(bf16[32,256]{1,0:T(8,128)(2,1)} %shard_map.100) | data formatting | bytes 32768 | tf_op jit(solution)/shard_map/reshape | solution.py:338

commit v4 on v3

--- a/solution.py
+++ b/solution.py
@@ -20,11 +20,11 @@
     tokens, task_emb, gen_in, gen_a, gen_b, w_gate, w_up, w_down, count, task,
     out,
     tok3_v, emb_v, gin_v, ga_v, gb_v, wg_v, wu_v, wd_v, cnt_v, tsk_v,
-    tok_v, tokp_v, wgp_v, wup_v, wdp_v, b_v,
+    tok_v, tokp_v, wgp_v, wup_v, wdp_v, wdz_v, wdzp_v, b_v,
     low_s, low1_r, low2_s, low2_r,
-    gate_s, up_f, up_s, gate_r, up_r, hid_v, mix_f, mix_s, mix_r, end_s, end_r,
-    known, load_sem, pair_ss, pair_rs, l1_ss, l1_rs, l2_ss, l2_rs,
-    g_ss, g_rs, u_ss, u_rs, h_ss, h_rs, m_ss, m_rs, e_ss, e_rs,
+    low_v, gate_s, gate_r, gate_f, gz_s, gz_r, up_f, up_s, up_r, hid_v, mix_f, mix_s, mix_r, end_s, end_r,
+    known, load_sem, pair_ss, pair_rs, wz_ss, wz_rs, wf_ss, wf_rs, l1_ss, l1_rs, l2_ss, l2_rs,
+    g_ss, g_rs, gz_ss, gz_rs, u_ss, u_rs, h_ss, h_rs, m_ss, m_rs, e_ss, e_rs,
 ):
     row = lax.axis_index("row")
     col = lax.axis_index("col")
@@ -34,6 +34,7 @@
     groups = count.shape[1]
     ranks = low_s.shape[1]
     mate = (row + 1 - 2 * core, col)
+    zmate = ((row + 8) % 16, col)
 
     def in_row(dz, dy, dk, sign=1):
         return ((z_lo + dz) % 2 * 4 + (y + sign * dy + 4) % 4) * 2 + (core + dk) % 2
@@ -43,6 +44,7 @@
 
     row_steps = [(dz, dy, dk) for dz in (1, 0) for dy in (2, 1, 3, 0) for dk in (1, 0)][:-1]
     col_steps = [(dz, dx) for dz in (2, 1, 3, 0) for dx in (2, 1, 3, 0)][:-1]
+    y_steps = (2, 1, 3)
     chip_steps = [(dz, dy) for dz in (1, 0) for dy in (2, 1, 3, 0)][:-1]
 
     bar = pltpu.get_barrier_semaphore()
@@ -130,30 +132,41 @@
         copy(wd_v, wdp_v, pair_ss.at[3], pair_rs.at[3], mate),
         copy(b_v.at[core], b_v.at[core], pair_ss.at[4], pair_rs.at[4], mate),
     ]
-    for n in range(4):
+    for n in range(2):
         pair[n].start()
+    units = wd_v.shape[0]
+    piece = units // 4
+    wz = [
+        copy(wd_v.at[pl.ds(n * piece, piece)], wdz_v.at[pl.ds(n * piece, piece)], wz_ss.at[n], wz_rs.at[n], zmate)
+        for n in range(4)
+    ]
+    wf = [
+        copy(
+            wdz_v.at[pl.ds(n * 2 * piece, 2 * piece)], wdzp_v.at[pl.ds(n * 2 * piece, 2 * piece)],
+            wf_ss.at[n], wf_rs.at[n], mate,
+        )
+        for n in range(2)
+    ]
+    wz[0].start()
+    wz[1].start()
+    pair[2].start()
     loads[6].wait()
     b_v[core] = dot(hyper, gb_v[...]).astype(BF16)
     pair[4].start()
+    pair[3].start()
 
     gate = dot(tok_v[mine, :], wg_v[...])
     pair[0].wait_recv()
     pair[1].wait_recv()
-    share = half // 8
+    block = half // 2
+    share = block // 4
     part = share // 2
-    units = gate.shape[1]
-    gate_s[...] = (gate + dot(tokp_v[...], wgp_v[...])).astype(BF16).reshape(2, 8, part, units)
-
-    def peer(dz, dy, sign=1):
-        return in_row(dz, dy, 0, sign) // 2
-
+    gate_s[...] = (gate + dot(tokp_v[...], wgp_v[...])).astype(BF16).reshape(2, 4, 2, part, units)
     gs = []
-    for n, (dz, dy) in enumerate(chip_steps):
-        i = peer(dz, dy)
-        gs.append(copy(gate_s.at[:, i], gate_r.at[n], g_ss.at[n], g_rs.at[n], (i * 2 + core, col)))
-    for n, (dz, dy) in enumerate(chip_steps):
-        if dz == 0:
-            gs[n].start()
+    for n, dy in enumerate(y_steps):
+        to = (y + dy) % 4
+        gs.append(copy(gate_s.at[:, to], gate_r.at[n], g_ss.at[n], g_rs.at[n], (in_row(0, dy, 0), col)))
+        gs[-1].start()
 
     low = low_s[core, pl.ds(chip * 2, 2)]
     for n in range(15):
@@ -165,68 +178,88 @@
     for n, (dz, dx) in enumerate(col_steps):
         l2.append(copy(low2_s, low2_r.at[n], l2_ss.at[n], l2_rs.at[n], (row, in_col(dz, dx))))
         l2[-1].start()
-    for n, (dz, dy) in enumerate(chip_steps):
-        if dz == 1:
-            gs[n].start()
+    wz[2].start()
+    wz[3].start()
 
     up = dot(tok_v[mine, :], wu_v[...])
     pair[2].wait_recv()
     up_f[...] = up + dot(tokp_v[...], wup_v[...])
     pair[4].wait_recv()
+    wz[0].wait_recv()
+    wz[1].wait_recv()
+    wf[0].start()
+    for c in gs:
+        c.wait_recv()
+
+    def gate_sum(q):
+        total = gate_s[q, y].astype(F32)
+        for n in range(3):
+            total = total + gate_r[n, q].astype(F32)
+        return total
+
+    gz_s[...] = gate_sum(1 - z_lo).astype(BF16)
+    gz = copy(gz_s, gz_r, gz_ss, gz_rs, zmate)
+    gz.start()
+    gate_f[...] = gate_sum(z_lo)
+
     b_all = b_v[...].reshape(2 * groups, units)
-    block = half // 2
-    mem = [member(core * half + a * block, block) for a in range(2)]
+    quarters = (1 - z_lo, z_lo)
+    mem = [member(core * half + q * block, block) for q in quarters]
     for n in range(15):
         l2[n].wait_recv()
         low = low + low2_r[n]
-    low = low.astype(BF16).astype(F32)
-    us = []
-    for a in range(2):
-        spread = jnp.concatenate([mem[a] * low[r, a : a + 1, :] for r in range(2)], axis=0).astype(BF16)
-        up = up_f[a * block : a * block + block, :] + dot(spread, b_all, ((0,), (0,)))
-        up_s[a] = up.astype(BF16).reshape(8, part, units)
-        us.append([])
+    low_v[...] = low.astype(BF16).astype(F32)
+    us = [[None] * 7 for _ in range(2)]
+
+    def send_up(a, across):
         for n, (dz, dy) in enumerate(chip_steps):
-            i = peer(dz, dy)
-            us[a].append(
-                copy(up_s.at[a, i], up_r.at[a, n], u_ss.at[a, n], u_rs.at[a, n], (i * 2 + core, col))
-            )
-            us[a][-1].start()
-
-    for n in range(7):
-        gs[n].wait_recv()
+            if dz == across:
+                src = up_s.at[(z_lo + dz) % 2, (y + dy) % 4, a]
+                to = (in_row(dz, dy, 0), col)
+                us[a][n] = copy(src, up_r.at[a, n], u_ss.at[a, n], u_rs.at[a, n], to)
+                us[a][n].start()
+
+    for t, q in enumerate(quarters):
+        spread = jnp.concatenate([mem[t] * low_v[r, pl.ds(q, 1), :] for r in range(2)], axis=0).astype(BF16)
+        here = pl.ds(pl.multiple_of(q * block, block), block)
+        up = up_f[here, :] + dot(spread, b_all, ((0,), (0,)))
+        up_s[q] = up.astype(BF16).reshape(4, 2, part, units)
+        send_up(0, 1 - t)
+    send_up(1, 1)
+    send_up(1, 0)
+    wz[2].wait_recv()
+    wz[3].wait_recv()
+    wf[1].start()
+
+    gz.wait_recv()
     hs = []
     for a in range(2):
-        gate = gate_s[a, chip].astype(F32)
-        for n in range(7):
-            gate = gate + gate_r[n, a].astype(F32)
-        act = jax.nn.silu(gate)
-        up = up_s[a, chip].astype(F32)
+        act = jax.nn.silu(gate_f[a] + gz_r[a].astype(F32))
+        up = up_s[z_lo, y, a].astype(F32)
         for n in range(7):
             us[a][n].wait_recv()
             up = up + up_r[a, n].astype(F32)
-        hid_v[a, chip] = (act * up).astype(BF16)
+        hid_v[a, y] = (act * up).astype(BF16)
         hs.append([])
-        for n, (dz, dy) in enumerate(chip_steps):
+        for n, dy in enumerate(y_steps):
             hs[a].append(
-                copy(
-                    hid_v.at[a, chip], hid_v.at[a, chip], h_ss.at[a, n], h_rs.at[a, n],
-                    (peer(dz, dy) * 2 + core, col),
-                )
+                copy(hid_v.at[a, y], hid_v.at[a, y], h_ss.at[a, n], h_rs.at[a, n], (in_row(0, dy, 0), col))
             )
             hs[a][-1].start()
 
     pair[3].wait_recv()
+    for c in wf:
+        c.wait_recv()
     ms = []
     for a in range(2):
-        for n, (dz, dy) in enumerate(chip_steps):
-            src = peer(dz, dy, -1)
+        for n, dy in enumerate(y_steps):
+            src = (y + 4 - dy) % 4
             copy(hid_v.at[a, src], hid_v.at[a, src], h_ss.at[a, n], h_rs.at[a, n], (row, col)).wait_recv()
-        hid = hid_v[a].reshape(block, units)
-        for k, w in enumerate((wd_v, wdp_v)):
-            mix = dot(hid, w[...])
-            mix_f[a, k] = mix.reshape(4, share, width)
-            mix_s[a, k] = mix.astype(BF16).reshape(4, share, width)
+        hid = hid_v[a].reshape(4 * part, units)
+        for k, w in enumerate((wd_v, wdp_v, wdz_v, wdzp_v)):
+            mix = dot(hid, w[...]).reshape(4, part, width)
+            mix_f[a, k] = mix
+            mix_s[a, k] = mix.astype(BF16)
         ms.append([])
         for n, d in enumerate((2, 1, 3)):
             ms[a].append(
@@ -234,39 +267,42 @@
             )
             ms[a][-1].start()
     es = []
+    to = (2 * core + z_lo) * 4 + x
+    stays = z_hi == 2 * core + z_lo
     for a in range(2):
-        to = 2 * core + a
-        here = z_hi == to
         mix = mix_f[a, :, x]
         for n in range(3):
             ms[a][n].wait_recv()
             mix = mix + mix_r[a, n].astype(F32)
         end_s[a] = mix.astype(BF16)
-        cross = copy(end_s.at[a, 1], end_r.at[z_hi], e_ss.at[a, 1], e_rs.at[z_hi], (mate[0], to * 4 + x))
-        same = copy(end_s.at[a, 0], end_r.at[z_hi], e_ss.at[a, 0], e_rs.at[z_hi], (row, to * 4 + x))
-        pl.when(jnp.logical_not(here))(same.start)
-        cross.start()
-
-        @pl.when(here)
+        for k, dev in enumerate((row, mate[0], zmate[0], in_row(1, 0, 1))):
+            c = copy(end_s.at[a, k], end_r.at[a, z_hi], e_ss.at[a, k], e_rs.at[a, z_hi], (dev, to))
+            if k == 0:
+                pl.when(jnp.logical_not(stays))(c.start)
+            else:
+                c.start()
+            es.append((k == 0, c))
+
+        @pl.when(stays)
         def _():
-            end_r[z_hi] = end_s[a, 0]
-
-        es.append((same, cross, here))
-
-    mine = z_hi // 2 == core
-    for s in range(4):
-        arrived = copy(end_r.at[s], end_r.at[s], e_ss.at[0, 0], e_rs.at[s], (row, col))
-        pl.when(jnp.logical_not(mine & (z_hi == s)))(arrived.wait_recv)
-    total = end_r[0].astype(F32)
-    for s in range(1, 4):
-        total = total + end_r[s].astype(F32)
-    out[...] = total.astype(BF16)
-
-    for c in l1 + l2 + pair + gs + us[0] + us[1] + hs[0] + hs[1] + ms[0] + ms[1]:
+            end_r[a, z_hi] = end_s[a, 0]
+
+    for a in range(2):
+        for s in range(4):
+            arrived = copy(end_r.at[a, s], end_r.at[a, s], e_ss.at[0, 0], e_rs.at[a, s], (row, col))
+            pl.when(jnp.logical_not(stays & (z_hi == s)))(arrived.wait_recv)
+        total = end_r[a, 0].astype(F32)
+        for s in range(1, 4):
+            total = total + end_r[a, s].astype(F32)
+        out[pl.ds(a * part, part), :] = total.astype(BF16)
+
+    for c in l1 + l2 + pair + wz + wf + gs + [gz] + us[0] + us[1] + hs[0] + hs[1] + ms[0] + ms[1]:
         c.wait_send()
-    for same, cross, here in es:
-        pl.when(jnp.logical_not(here))(same.wait_send)
-        cross.wait_send()
+    for local, c in es:
+        if local:
+            pl.when(jnp.logical_not(stays))(c.wait_send)
+        else:
+            c.wait_send()
 
 
 def shards(tokens, task_emb, gen_in, gen_a, gen_b, w_gate, w_up, w_down, group_count, group_task):
@@ -299,30 +335,52 @@
         vm((width, units), BF16),
         vm((width, units), BF16),
         vm((units, width), BF16),
+        vm((units, width), BF16),
+        vm((units, width), BF16),
         vm((2, groups, units), BF16),
         vm((2, ranks, 2, half // 2), F32),
         vm((15, 2, 2, half // 2), F32),
         vm((2, 2, half // 2), F32),
         vm((15, 2, 2, half // 2), F32),
-        vm((2, 8, part, units), BF16),
+        vm((2, 2, half // 2), F32),
+        vm((2, 4, 2, part, units), BF16),
+        vm((3, 2, 2, part, units), BF16),
+        vm((2, part, units), F32),
+        vm((2, part, units), BF16),
+        vm((2, part, units), BF16),
         vm((half, units), F32),
-        vm((2, 8, part, units), BF16),
-        vm((7, 2, part, units), BF16),
+        vm((2, 4, 2, part, units), BF16),
         vm((2, 7, part, units), BF16),
-        vm((2, 8, part, units), BF16),
-        vm((2, 2, 4, share, width), F32),
-        vm((2, 2, 4, share, width), BF16),
-        vm((2, 3, 2, share, width), BF16),
-        vm((2, 2, share, width), BF16),
-        vm((4, share, width), BF16),
+        vm((2, 4, part, units), BF16),
+        vm((2, 4, 4, part, width), F32),
+        vm((2, 4, 4, part, width), BF16),
+        vm((2, 3, 4, part, width), BF16),
+        vm((2, 4, part, width), BF16),
+        vm((2, 4, part, width), BF16),
         pltpu.SemaphoreType.REGULAR,
-    ]
-    scratch += [
-        dma(n)
-        for n in (
-            (10,), (5,), (5,), (15,), (15,), (15,), (15,),
-            (7,), (7,), (2, 7), (2, 7), (2, 7), (2, 7), (2, 3), (2, 3), (2, 2), (4,),
-        )
+        dma((10,)),
+        dma((5,)),
+        dma((5,)),
+        dma((4,)),
+        dma((4,)),
+        dma((2,)),
+        dma((2,)),
+        dma((15,)),
+        dma((15,)),
+        dma((15,)),
+        dma((15,)),
+        dma((3,)),
+        dma((3,)),
+        dma,
+        dma,
+        dma((2, 7)),
+        dma((2, 7)),
+        dma((2, 3)),
+        dma((2, 3)),
+        dma((2, 3)),
+        dma((2, 3)),
+        dma((2, 4)),
+        dma((2, 4)),
     ]
     any_spec = pl.BlockSpec(memory_space=pl.ANY)
     out = pl.pallas_call(
@@ -332,9 +390,9 @@
         out_specs=pl.BlockSpec(memory_space=pltpu.VMEM),
         scratch_shapes=scratch,
         compiler_params=pltpu.CompilerParams(
-            collective_id=0, has_side_effects=True, vmem_limit_bytes=56 * 1024 * 1024
+            collective_id=0, has_side_effects=True, vmem_limit_bytes=32 * 1024 * 1024
         ),
-    )(*args)
+    )(*[pltpu.with_memory_space_constraint(a, pltpu.HBM) for a in args])
     return out.reshape(share // draft, draft, width)
 
 

time: 43.8 us -> 44.9 us (1.025)
  Pallas kernels: 42.3 us -> 44.2 us
  local copies, waits for them, and re-layouts: 1.34 us -> 0.62 us
    pallas_call x1, Pallas kernels: 42.3 us -> 44.2 us  [shards(): pl.pallas_call(kernel, out_shape=jax.ShapeDtypeStruct((share, width), BF1...]
    reshape x1, local copies, waits for them, and re-layouts: 1.34 us -> 0.62 us  [shards(): return out.reshape(share // draft, draft, width)]
where the time goes in v4:
time: 44.9 us
  Pallas kernels  44.2 us (98%)
  local copies, waits for them, and re-layouts  0.62 us (1%)
    pallas_call x1, Pallas kernels, shards(): pl.pallas_call(kernel, out_shape=jax.ShapeDtypeStruct((share, width), BF1...  44.2 us

profile of v4, /device:TPU:1, one launch (start us, length us, event | category | flops | bytes accessed | tf_op | source)
XLA Modules:
  0.0 44.9 jit_solution(3695450516007640654)
XLA Ops:
  0.0 44.2 %shard_map.100 = bf16[32,256]{1,0:T(8,128)(2,1)S(1)} custom-call(bf16[256,2,256]{2,1,0:T(2,128)(2,1)} %tokens.1, bf16[512,1024]{1,0:T(8,128)(2,1)} %task_emb.1, bf16[1024,512]{1,0:T(8,128)(2,1)} %gen_in.1, bf16[256,512]{1,0:T(8,128)(2,1)} %bitcast.7, bf16[512,896]{1,0:T(8,128)(2,1)} %bitcast.6, bf16[256,896]{1,0:T(8,128)(2,1)} %w_gate.1, ...), custom_call_target="tpu_custom_call" | custom-call | tf_op jit(solution)/shard_map/pallas_call | solution.py:386
  44.2 0.6 %reshape.19 = bf16[16,2,256]{2,1,0:T(2,128)(2,1)} reshape(bf16[32,256]{1,0:T(8,128)(2,1)S(1)} %shard_map.100) | data formatting | bytes 32768 | tf_op jit(solution)/shard_map/reshape | solution.py:396

commit v5 on v3

--- a/solution.py
+++ b/solution.py
@@ -332,9 +332,9 @@
         out_specs=pl.BlockSpec(memory_space=pltpu.VMEM),
         scratch_shapes=scratch,
         compiler_params=pltpu.CompilerParams(
-            collective_id=0, has_side_effects=True, vmem_limit_bytes=56 * 1024 * 1024
+            collective_id=0, has_side_effects=True, vmem_limit_bytes=32 * 1024 * 1024
         ),
-    )(*args)
+    )(*[pltpu.with_memory_space_constraint(a, pltpu.HBM) for a in args])
     return out.reshape(share // draft, draft, width)
 
 

time: 43.8 us -> 42.3 us (0.966)
  local copies, waits for them, and re-layouts: 1.34 us -> 0.62 us
  Pallas kernels: 42.3 us -> 41.6 us
    reshape x1, local copies, waits for them, and re-layouts: 1.34 us -> 0.62 us  [shards(): return out.reshape(share // draft, draft, width)]
    pallas_call x1, Pallas kernels: 42.3 us -> 41.6 us  [shards(): pl.pallas_call(kernel, out_shape=jax.ShapeDtypeStruct((share, width), BF1...]
where the time goes in v5:
time: 42.3 us
  Pallas kernels  41.6 us (98%)
  local copies, waits for them, and re-layouts  0.62 us (1%)
    pallas_call x1, Pallas kernels, shards(): pl.pallas_call(kernel, out_shape=jax.ShapeDtypeStruct((share, width), BF1...  41.6 us

profile of v5, /device:TPU:1, one launch (start us, length us, event | category | flops | bytes accessed | tf_op | source)
XLA Modules:
  0.0 42.3 jit_solution(9980999339515469833)
XLA Ops:
  0.0 41.6 %shard_map.100 = bf16[32,256]{1,0:T(8,128)(2,1)S(1)} custom-call(bf16[256,2,256]{2,1,0:T(2,128)(2,1)} %tokens.1, bf16[512,1024]{1,0:T(8,128)(2,1)} %task_emb.1, bf16[1024,512]{1,0:T(8,128)(2,1)} %gen_in.1, bf16[256,512]{1,0:T(8,128)(2,1)} %bitcast.7, bf16[512,896]{1,0:T(8,128)(2,1)} %bitcast.6, bf16[256,896]{1,0:T(8,128)(2,1)} %w_gate.1, ...), custom_call_target="tpu_custom_call" | custom-call | tf_op jit(solution)/shard_map/pallas_call | solution.py:328
  41.6 0.6 %reshape.19 = bf16[16,2,256]{2,1,0:T(2,128)(2,1)} reshape(bf16[32,256]{1,0:T(8,128)(2,1)S(1)} %shard_map.100) | data formatting | bytes 32768 | tf_op jit(solution)/shard_map/reshape | solution.py:338

commit v6 on v5

--- a/solution.py
+++ b/solution.py
@@ -20,10 +20,10 @@
     tokens, task_emb, gen_in, gen_a, gen_b, w_gate, w_up, w_down, count, task,
     out,
     tok3_v, emb_v, gin_v, ga_v, gb_v, wg_v, wu_v, wd_v, cnt_v, tsk_v,
-    tok_v, tokp_v, wgp_v, wup_v, wdp_v, b_v,
+    tok_v, tokp_v, wgp_v, wup_v, wdp_v, bs_s, bs_r,
     low_s, low1_r, low2_s, low2_r,
-    gate_s, up_f, up_s, gate_r, up_r, hid_v, mix_f, mix_s, mix_r, end_s, end_r,
-    known, load_sem, pair_ss, pair_rs, l1_ss, l1_rs, l2_ss, l2_rs,
+    gate_s, up_s, gate_r, up_r, hid_v, mix_f, mix_s, mix_r, end_s, end_r,
+    known, load_sem, pair_ss, pair_rs, l1_ss, l1_rs, l2_ss, l2_rs, b_ss, b_rs,
     g_ss, g_rs, u_ss, u_rs, h_ss, h_rs, m_ss, m_rs, e_ss, e_rs,
 ):
     row = lax.axis_index("row")
@@ -32,7 +32,7 @@
     z_hi, x = col // 4, col % 4
     chip = row // 2
     groups = count.shape[1]
-    ranks = low_s.shape[1]
+    ranks = bs_r.shape[0]
     mate = (row + 1 - 2 * core, col)
 
     def in_row(dz, dy, dk, sign=1):
@@ -57,8 +57,8 @@
         pltpu.make_async_copy(src, dst, load_sem.at[n])
         for n, (src, dst) in enumerate(
             [
-                (task, tsk_v), (task_emb, emb_v), (gen_in, gin_v), (count, cnt_v), (gen_a, ga_v),
-                (tokens, tok3_v), (gen_b, gb_v), (w_gate, wg_v), (w_up, wu_v), (w_down, wd_v),
+                (task, tsk_v), (task_emb, emb_v), (gen_in, gin_v), (count, cnt_v), (gen_b, gb_v), (gen_a, ga_v),
+                (tokens, tok3_v), (w_gate, wg_v), (w_up, wu_v), (w_down, wd_v),
             ]
         )
     ]
@@ -83,29 +83,59 @@
 
     loads[3].wait()
     cnt = cnt_v[...].astype(F32)
+    cnt_of = jnp.sum(jnp.where(gi == gj, cnt, 0.0), axis=1, keepdims=True)
     ends = jnp.sum(jnp.where(gj <= gi, cnt, 0.0), axis=1, keepdims=True)
-    starts = ends - jnp.sum(jnp.where(gj == gi, cnt, 0.0), axis=1, keepdims=True)
-
-    def member(first, width):
-        request = (lax.broadcasted_iota(jnp.int32, (groups, width), 1) + first) // 2
-        request = request.astype(F32)
-        return jnp.where((request >= starts) & (request < ends), 1.0, 0.0)
-
-    loads[4].wait()
-    fac_a = dot(ga_v[...], hyper, ((1,), (1,))).astype(BF16)
+    starts = ends - cnt_of
+    ends_t = jnp.sum(jnp.where(gi <= gj, cnt_of, 0.0), axis=0, keepdims=True)
+    starts_t = ends_t - cnt
+
     n_tok = tok_v.shape[0]
     width = tok_v.shape[1]
-    slab = fac_a.shape[0] // ranks
-    a_of = dot(fac_a, member(0, n_tok).astype(BF16))
-    which = lax.broadcasted_iota(jnp.int32, (slab * ranks, width), 0) // ranks + col * slab
-    sel = jnp.where(lax.broadcasted_iota(jnp.int32, (slab * ranks, width), 1) == which, 1.0, 0.0)
+    half = n_tok // 2
+    units = wd_v.shape[0]
+    block = half // 2
+    share = half // 8
+    part = share // 2
+    drafts = 2
+    own = part // drafts
+
+    def iota(rows, cols, dim):
+        return lax.broadcasted_iota(jnp.int32, (rows, cols), dim)
+
+    m = iota(groups, n_tok // drafts, 1)
+    request = m // 128 * 128 + m // own % 2 * 64 + m // (2 * own) % 8 * own + m % own
+    request = request.astype(F32)
+    member = jnp.where((request >= starts) & (request < ends), 1.0, 0.0).astype(BF16)
+    loads[4].wait()
+    fac_b = dot(hyper, gb_v[...]).astype(BF16)
+    bs_s[...] = dot(member, fac_b, ((0,), (0,))).astype(BF16).reshape(2, 8, 2 * own, units)
+
     loads[5].wait()
+    fac_a = dot(hyper, ga_v[...], ((1,), (1,))).astype(BF16)
+    cols = fac_a.shape[1]
+    request = (iota(n_tok, groups, 0) // drafts).astype(F32)
+    member = jnp.where((request >= starts_t) & (request < ends_t), 1.0, 0.0).astype(BF16)
+    a_of = dot(member, fac_a)
+    sel = iota(width, cols, 0) == iota(width, cols, 1) // ranks + col * (cols // ranks)
+    loads[6].wait()
     tok_v[...] = tok3_v[...].reshape(n_tok, width)
-    t_of = dot(sel.astype(BF16), tok_v[...], ((1,), (1,)))
-    low = jnp.sum((a_of * t_of).reshape(slab, ranks, n_tok), axis=0)
+    prod = a_of * dot(tok_v[...], jnp.where(sel, 1.0, 0.0).astype(BF16))
+    high = prod.astype(BF16)
+    rest = (prod - high.astype(F32)).astype(BF16)
+    lanes = ranks * 2 * own
+    place = jnp.where(iota(cols, lanes, 0) % ranks == iota(cols, lanes, 1) // (2 * own), 1.0, 0.0).astype(BF16)
+    t = iota(n_tok, lanes, 0)
+    at = t // block % 2 * own + t // drafts % own
+    spread = jnp.where(at == iota(n_tok, lanes, 1) % (2 * own), dot(high, place) + dot(rest, place), 0.0)
+    t = iota(32, n_tok, 1)
+    to_row = t // half * 16 + t // part % 8 * drafts + t % drafts == iota(32, n_tok, 0)
+    low = lax.dot_general(
+        jnp.where(to_row, 1.0, 0.0), spread, (((1,), (0,)), ((), ())),
+        precision=lax.Precision.HIGHEST, preferred_element_type=F32,
+    )
     for h in range(2):
-        for q in range(2):
-            low_s[h, :, q, :] = low[:, h * 256 + q * 128 : h * 256 + q * 128 + 128]
+        for i in range(8):
+            low_s[h, i] = low[h * 16 + i * 2 : h * 16 + i * 2 + 2, :]
 
     pl.semaphore_wait(bar, 21)
     for d in (2, 1, 3):
@@ -114,11 +144,8 @@
     l1 = []
     for n, (dz, dy, dk) in enumerate(row_steps):
         to = in_row(dz, dy, dk)
-        l1.append(
-            copy(low_s.at[to % 2, pl.ds(to // 2 * 2, 2)], low1_r.at[n], l1_ss.at[n], l1_rs.at[n], (to, col))
-        )
+        l1.append(copy(low_s.at[to % 2, to // 2], low1_r.at[n], l1_ss.at[n], l1_rs.at[n], (to, col)))
         l1[-1].start()
-    half = tok_v.shape[0] // 2
     other = pl.ds(pl.multiple_of((1 - core) * half, half), half)
     mine = pl.ds(pl.multiple_of(core * half, half), half)
     for n in (7, 8, 9):
@@ -128,20 +155,20 @@
         copy(wg_v, wgp_v, pair_ss.at[1], pair_rs.at[1], mate),
         copy(wu_v, wup_v, pair_ss.at[2], pair_rs.at[2], mate),
         copy(wd_v, wdp_v, pair_ss.at[3], pair_rs.at[3], mate),
-        copy(b_v.at[core], b_v.at[core], pair_ss.at[4], pair_rs.at[4], mate),
     ]
-    for n in range(4):
-        pair[n].start()
-    loads[6].wait()
-    b_v[core] = dot(hyper, gb_v[...]).astype(BF16)
-    pair[4].start()
+    for c in pair[:3]:
+        c.start()
+    bs = []
+    for n, (dz, dy, dk) in enumerate(row_steps):
+        to = in_row(dz, dy, dk)
+        bs.append(copy(bs_s.at[to % 2, to // 2], bs_r.at[row], b_ss.at[n], b_rs.at[row], (to, col)))
+        bs[-1].start()
+    pair[3].start()
+    bs_r[row] = bs_s[core, chip]
 
     gate = dot(tok_v[mine, :], wg_v[...])
     pair[0].wait_recv()
     pair[1].wait_recv()
-    share = half // 8
-    part = share // 2
-    units = gate.shape[1]
     gate_s[...] = (gate + dot(tokp_v[...], wgp_v[...])).astype(BF16).reshape(2, 8, part, units)
 
     def peer(dz, dy, sign=1):
@@ -154,8 +181,11 @@
     for n, (dz, dy) in enumerate(chip_steps):
         if dz == 0:
             gs[n].start()
-
-    low = low_s[core, pl.ds(chip * 2, 2)]
+    up = dot(tok_v[mine, :], wu_v[...])
+    pair[2].wait_recv()
+    up_s[...] = (up + dot(tokp_v[...], wup_v[...])).astype(BF16).reshape(2, 8, part, units)
+
+    low = low_s[core, chip]
     for n in range(15):
         l1[n].wait_recv()
         low = low + low1_r[n]
@@ -168,23 +198,8 @@
     for n, (dz, dy) in enumerate(chip_steps):
         if dz == 1:
             gs[n].start()
-
-    up = dot(tok_v[mine, :], wu_v[...])
-    pair[2].wait_recv()
-    up_f[...] = up + dot(tokp_v[...], wup_v[...])
-    pair[4].wait_recv()
-    b_all = b_v[...].reshape(2 * groups, units)
-    block = half // 2
-    mem = [member(core * half + a * block, block) for a in range(2)]
-    for n in range(15):
-        l2[n].wait_recv()
-        low = low + low2_r[n]
-    low = low.astype(BF16).astype(F32)
     us = []
     for a in range(2):
-        spread = jnp.concatenate([mem[a] * low[r, a : a + 1, :] for r in range(2)], axis=0).astype(BF16)
-        up = up_f[a * block : a * block + block, :] + dot(spread, b_all, ((0,), (0,)))
-        up_s[a] = up.astype(BF16).reshape(8, part, units)
         us.append([])
         for n, (dz, dy) in enumerate(chip_steps):
             i = peer(dz, dy)
@@ -192,6 +207,18 @@
                 copy(up_s.at[a, i], up_r.at[a, n], u_ss.at[a, n], u_rs.at[a, n], (i * 2 + core, col))
             )
             us[a][-1].start()
+
+    for n in range(15):
+        l2[n].wait_recv()
+        low = low + low2_r[n]
+    low = low.astype(BF16).astype(F32)
+    m = iota(share, lanes, 0)
+    low = jnp.where(m % 2 == 0, low[0:1, :], low[1:2, :])
+    low = jnp.where(m // drafts == iota(share, lanes, 1) % (2 * own), low, 0.0).astype(BF16)
+    for n, (dz, dy, dk) in enumerate(row_steps):
+        src = in_row(dz, dy, dk, -1)
+        copy(bs_s.at[0, 0], bs_r.at[src], b_ss.at[n], b_rs.at[src], (row, col)).wait_recv()
+    lora = dot(low, bs_r[...].reshape(lanes, units))
 
     for n in range(7):
         gs[n].wait_recv()
@@ -201,7 +228,7 @@
         for n in range(7):
             gate = gate + gate_r[n, a].astype(F32)
         act = jax.nn.silu(gate)
-        up = up_s[a, chip].astype(F32)
+        up = up_s[a, chip].astype(F32) + lora[a * part : a * part + part, :]
         for n in range(7):
             us[a][n].wait_recv()
             up = up + up_r[a, n].astype(F32)
@@ -262,7 +289,7 @@
         total = total + end_r[s].astype(F32)
     out[...] = total.astype(BF16)
 
-    for c in l1 + l2 + pair + gs + us[0] + us[1] + hs[0] + hs[1] + ms[0] + ms[1]:
+    for c in l1 + l2 + pair + bs + gs + us[0] + us[1] + hs[0] + hs[1] + ms[0] + ms[1]:
         c.wait_send()
     for same, cross, here in es:
         pl.when(jnp.logical_not(here))(same.wait_send)
@@ -299,13 +326,13 @@
         vm((width, units), BF16),
         vm((width, units), BF16),
         vm((units, width), BF16),
-        vm((2, groups, units), BF16),
-        vm((2, ranks, 2, half // 2), F32),
-        vm((15, 2, 2, half // 2), F32),
-        vm((2, 2, half // 2), F32),
-        vm((15, 2, 2, half // 2), F32),
         vm((2, 8, part, units), BF16),
-        vm((half, units), F32),
+        vm((ranks, part, units), BF16),
+        vm((2, 8, 2, ranks * part), F32),
+        vm((15, 2, ranks * part), F32),
+        vm((2, ranks * part), F32),
+        vm((15, 2, ranks * part), F32),
+        vm((2, 8, part, units), BF16),
         vm((2, 8, part, units), BF16),
         vm((7, 2, part, units), BF16),
         vm((2, 7, part, units), BF16),
@@ -320,7 +347,7 @@
     scratch += [
         dma(n)
         for n in (
-            (10,), (5,), (5,), (15,), (15,), (15,), (15,),
+            (10,), (4,), (4,), (15,), (15,), (15,), (15,), (15,), (16,),
             (7,), (7,), (2, 7), (2, 7), (2, 7), (2, 7), (2, 3), (2, 3), (2, 2), (4,),
         )
     ]

time: 42.3 us -> 45.3 us (1.071)
  Pallas kernels: 41.6 us -> 44.6 us
    pallas_call x1, Pallas kernels: 41.6 us -> 44.6 us  [shards(): pl.pallas_call(kernel, out_shape=jax.ShapeDtypeStruct((share, width), BF1...]
where the time goes in v6:
time: 45.3 us; the launch traced here: 45.2 us
  Pallas kernels  44.6 us (98%)
  local copies, waits for them, and re-layouts  0.62 us (1%)
    pallas_call x1, Pallas kernels, shards(): pl.pallas_call(kernel, out_shape=jax.ShapeDtypeStruct((share, width), BF1...  44.6 us

profile of v6, /device:TPU:1, one launch (start us, length us, event | category | flops | bytes accessed | tf_op | source)
XLA Modules:
  0.0 45.2 jit_solution(15176846998181301419)
XLA Ops:
  0.0 44.6 %shard_map.100 = bf16[32,256]{1,0:T(8,128)(2,1)S(1)} custom-call(bf16[256,2,256]{2,1,0:T(2,128)(2,1)} %tokens.1, bf16[512,1024]{1,0:T(8,128)(2,1)} %task_emb.1, bf16[1024,512]{1,0:T(8,128)(2,1)} %gen_in.1, bf16[256,512]{1,0:T(8,128)(2,1)} %bitcast.7, bf16[512,896]{1,0:T(8,128)(2,1)} %bitcast.6, bf16[256,896]{1,0:T(8,128)(2,1)} %w_gate.1, ...), custom_call_target="tpu_custom_call" | custom-call | tf_op jit(solution)/shard_map/pallas_call | solution.py:355
  44.6 0.6 %reshape.19 = bf16[16,2,256]{2,1,0:T(2,128)(2,1)} reshape(bf16[32,256]{1,0:T(8,128)(2,1)S(1)} %shard_map.100) | data formatting | bytes 32768 | tf_op jit(solution)/shard_map/reshape | solution.py:365

commit v7 on v5

--- a/solution.py
+++ b/solution.py
@@ -87,21 +87,24 @@
     starts = ends - jnp.sum(jnp.where(gj == gi, cnt, 0.0), axis=1, keepdims=True)
 
     def member(first, width):
-        request = (lax.broadcasted_iota(jnp.int32, (groups, width), 1) + first) // 2
-        request = request.astype(F32)
+        m = lax.broadcasted_iota(jnp.int32, (groups, width), 1) + first
+        token = m // 64 % 4 * 128 + m // 16 % 4 * 32 + m // 256 * 16 + m % 16
+        request = (token // 2).astype(F32)
         return jnp.where((request >= starts) & (request < ends), 1.0, 0.0)
 
     loads[4].wait()
     fac_a = dot(ga_v[...], hyper, ((1,), (1,))).astype(BF16)
-    n_tok = tok_v.shape[0]
-    width = tok_v.shape[1]
+    half, width = tok_v.shape[1:]
+    n_tok = 2 * half
     slab = fac_a.shape[0] // ranks
     a_of = dot(fac_a, member(0, n_tok).astype(BF16))
     which = lax.broadcasted_iota(jnp.int32, (slab * ranks, width), 0) // ranks + col * slab
     sel = jnp.where(lax.broadcasted_iota(jnp.int32, (slab * ranks, width), 1) == which, 1.0, 0.0)
     loads[5].wait()
-    tok_v[...] = tok3_v[...].reshape(n_tok, width)
-    t_of = dot(sel.astype(BF16), tok_v[...], ((1,), (1,)))
+    tok = tok3_v[...].reshape(16, 2, n_tok // 32, width)
+    for k in range(2):
+        tok_v[k] = tok[:, k].reshape(half, width)
+    t_of = dot(sel.astype(BF16), tok_v[...].reshape(n_tok, width), ((1,), (1,)))
     low = jnp.sum((a_of * t_of).reshape(slab, ranks, n_tok), axis=0)
     for h in range(2):
         for q in range(2):
@@ -118,13 +121,10 @@
             copy(low_s.at[to % 2, pl.ds(to // 2 * 2, 2)], low1_r.at[n], l1_ss.at[n], l1_rs.at[n], (to, col))
         )
         l1[-1].start()
-    half = tok_v.shape[0] // 2
-    other = pl.ds(pl.multiple_of((1 - core) * half, half), half)
-    mine = pl.ds(pl.multiple_of(core * half, half), half)
     for n in (7, 8, 9):
         loads[n].wait()
     pair = [
-        copy(tok_v.at[other], tokp_v, pair_ss.at[0], pair_rs.at[0], mate),
+        copy(tok_v.at[1 - core], tokp_v, pair_ss.at[0], pair_rs.at[0], mate),
         copy(wg_v, wgp_v, pair_ss.at[1], pair_rs.at[1], mate),
         copy(wu_v, wup_v, pair_ss.at[2], pair_rs.at[2], mate),
         copy(wd_v, wdp_v, pair_ss.at[3], pair_rs.at[3], mate),
@@ -136,13 +136,12 @@
     b_v[core] = dot(hyper, gb_v[...]).astype(BF16)
     pair[4].start()
 
-    gate = dot(tok_v[mine, :], wg_v[...])
+    gate = dot(tok_v[core], wg_v[...])
     pair[0].wait_recv()
     pair[1].wait_recv()
-    share = half // 8
-    part = share // 2
+    part = half // 32
     units = gate.shape[1]
-    gate_s[...] = (gate + dot(tokp_v[...], wgp_v[...])).astype(BF16).reshape(2, 8, part, units)
+    gate_s[...] = (gate + dot(tokp_v[...], wgp_v[...])).astype(BF16).reshape(4, 8, part, units)
 
     def peer(dz, dy, sign=1):
         return in_row(dz, dy, 0, sign) // 2
@@ -169,7 +168,7 @@
         if dz == 1:
             gs[n].start()
 
-    up = dot(tok_v[mine, :], wu_v[...])
+    up = dot(tok_v[core], wu_v[...])
     pair[2].wait_recv()
     up_f[...] = up + dot(tokp_v[...], wup_v[...])
     pair[4].wait_recv()
@@ -181,88 +180,108 @@
         low = low + low2_r[n]
     low = low.astype(BF16).astype(F32)
     us = []
+    for q in range(4):
+        us.append([])
+        for n, (dz, dy) in enumerate(chip_steps):
+            i = peer(dz, dy)
+            us[q].append(
+                copy(up_s.at[q, i], up_r.at[q, n], u_ss.at[q, n], u_rs.at[q, n], (i * 2 + core, col))
+            )
     for a in range(2):
         spread = jnp.concatenate([mem[a] * low[r, a : a + 1, :] for r in range(2)], axis=0).astype(BF16)
         up = up_f[a * block : a * block + block, :] + dot(spread, b_all, ((0,), (0,)))
-        up_s[a] = up.astype(BF16).reshape(8, part, units)
-        us.append([])
-        for n, (dz, dy) in enumerate(chip_steps):
-            i = peer(dz, dy)
-            us[a].append(
-                copy(up_s.at[a, i], up_r.at[a, n], u_ss.at[a, n], u_rs.at[a, n], (i * 2 + core, col))
-            )
-            us[a][-1].start()
+        up_s[2 * a : 2 * a + 2] = up.astype(BF16).reshape(2, 8, part, units)
+        for q in (0, 1) if a == 0 else (2,):
+            for c in us[q]:
+                c.start()
 
     for n in range(7):
         gs[n].wait_recv()
-    hs = []
-    for a in range(2):
-        gate = gate_s[a, chip].astype(F32)
+    hs, ms, es = [], [], []
+
+    def hidden(q):
+        gate = gate_s[q, chip].astype(F32)
         for n in range(7):
-            gate = gate + gate_r[n, a].astype(F32)
+            gate = gate + gate_r[n, q].astype(F32)
         act = jax.nn.silu(gate)
-        up = up_s[a, chip].astype(F32)
+        up = up_s[q, chip].astype(F32)
         for n in range(7):
-            us[a][n].wait_recv()
-            up = up + up_r[a, n].astype(F32)
-        hid_v[a, chip] = (act * up).astype(BF16)
+            us[q][n].wait_recv()
+            up = up + up_r[q, n].astype(F32)
+        hid_v[q, chip] = (act * up).astype(BF16)
         hs.append([])
         for n, (dz, dy) in enumerate(chip_steps):
-            hs[a].append(
+            hs[q].append(
                 copy(
-                    hid_v.at[a, chip], hid_v.at[a, chip], h_ss.at[a, n], h_rs.at[a, n],
+                    hid_v.at[q, chip], hid_v.at[q, chip], h_ss.at[q, n], h_rs.at[q, n],
                     (peer(dz, dy) * 2 + core, col),
                 )
             )
-            hs[a][-1].start()
-
-    pair[3].wait_recv()
-    ms = []
-    for a in range(2):
+            hs[q][-1].start()
+
+    rows = half // 16
+
+    def partial(q):
         for n, (dz, dy) in enumerate(chip_steps):
             src = peer(dz, dy, -1)
-            copy(hid_v.at[a, src], hid_v.at[a, src], h_ss.at[a, n], h_rs.at[a, n], (row, col)).wait_recv()
-        hid = hid_v[a].reshape(block, units)
+            copy(hid_v.at[q, src], hid_v.at[q, src], h_ss.at[q, n], h_rs.at[q, n], (row, col)).wait_recv()
+        hid = hid_v[q].reshape(8 * part, units)
         for k, w in enumerate((wd_v, wdp_v)):
-            mix = dot(hid, w[...])
-            mix_f[a, k] = mix.reshape(4, share, width)
-            mix_s[a, k] = mix.astype(BF16).reshape(4, share, width)
+            mix = dot(hid, w[...]).reshape(4, rows, width)
+            mix_f[q, k] = mix
+            mix_s[q, k] = mix.astype(BF16)
         ms.append([])
         for n, d in enumerate((2, 1, 3)):
-            ms[a].append(
-                copy(mix_s.at[a, :, (x + d) % 4], mix_r.at[a, n], m_ss.at[a, n], m_rs.at[a, n], (row, in_col(0, d)))
+            ms[q].append(
+                copy(mix_s.at[q, :, (x + d) % 4], mix_r.at[q, n], m_ss.at[q, n], m_rs.at[q, n], (row, in_col(0, d)))
             )
-            ms[a][-1].start()
-    es = []
-    for a in range(2):
-        to = 2 * core + a
-        here = z_hi == to
-        mix = mix_f[a, :, x]
+            ms[q][-1].start()
+
+    def end(q):
+        here = z_hi == q
+        mix = mix_f[q, :, x]
         for n in range(3):
-            ms[a][n].wait_recv()
-            mix = mix + mix_r[a, n].astype(F32)
-        end_s[a] = mix.astype(BF16)
-        cross = copy(end_s.at[a, 1], end_r.at[z_hi], e_ss.at[a, 1], e_rs.at[z_hi], (mate[0], to * 4 + x))
-        same = copy(end_s.at[a, 0], end_r.at[z_hi], e_ss.at[a, 0], e_rs.at[z_hi], (row, to * 4 + x))
+            ms[q][n].wait_recv()
+            mix = mix + mix_r[q, n].astype(F32)
+        end_s[q] = mix.astype(BF16)
+        slot = end_r.at[core, z_hi]
+        cross = copy(end_s.at[q, 1], slot, e_ss.at[q, 1], e_rs.at[core, z_hi], (mate[0], q * 4 + x))
+        same = copy(end_s.at[q, 0], slot, e_ss.at[q, 0], e_rs.at[core, z_hi], (row, q * 4 + x))
         pl.when(jnp.logical_not(here))(same.start)
         cross.start()
 
         @pl.when(here)
         def _():
-            end_r[z_hi] = end_s[a, 0]
+            end_r[core, z_hi] = end_s[q, 0]
 
         es.append((same, cross, here))
 
-    mine = z_hi // 2 == core
-    for s in range(4):
-        arrived = copy(end_r.at[s], end_r.at[s], e_ss.at[0, 0], e_rs.at[s], (row, col))
-        pl.when(jnp.logical_not(mine & (z_hi == s)))(arrived.wait_recv)
-    total = end_r[0].astype(F32)
-    for s in range(1, 4):
-        total = total + end_r[s].astype(F32)
-    out[...] = total.astype(BF16)
-
-    for c in l1 + l2 + pair + gs + us[0] + us[1] + hs[0] + hs[1] + ms[0] + ms[1]:
+    hidden(0)
+    for c in us[3]:
+        c.start()
+    hidden(1)
+    hidden(2)
+    pair[3].wait_recv()
+    partial(0)
+    hidden(3)
+    partial(1)
+    end(0)
+    partial(2)
+    end(1)
+    partial(3)
+    end(2)
+    end(3)
+
+    for k in range(2):
+        for s in range(4):
+            arrived = copy(end_r.at[k, s], end_r.at[k, s], e_ss.at[0, 0], e_rs.at[k, s], (row, col))
+            pl.when(jnp.logical_not((core == k) & (z_hi == s)))(arrived.wait_recv)
+        total = end_r[k, 0].astype(F32)
+        for s in range(1, 4):
+            total = total + end_r[k, s].astype(F32)
+        out[k * rows : k * rows + rows, :] = total.astype(BF16)
+
+    for c in l1 + l2 + pair + gs + sum(us, []) + sum(hs, []) + sum(ms, []):
         c.wait_send()
     for same, cross, here in es:
         pl.when(jnp.logical_not(here))(same.wait_send)
@@ -277,7 +296,8 @@
     n_tok = batch * draft
     half = n_tok // 2
     share = half // 8
-    part = share // 2
+    part = half // 32
+    rows = half // 16
     vm = pltpu.VMEM
     dma = pltpu.SemaphoreType.DMA
     args = (
@@ -294,7 +314,7 @@
     )
     scratch = [vm(a.shape, a.dtype) for a in args]
     scratch += [
-        vm((n_tok, width), BF16),
+        vm((2, half, width), BF16),
         vm((half, width), BF16),
         vm((width, units), BF16),
         vm((width, units), BF16),
@@ -304,24 +324,24 @@
         vm((15, 2, 2, half // 2), F32),
         vm((2, 2, half // 2), F32),
         vm((15, 2, 2, half // 2), F32),
-        vm((2, 8, part, units), BF16),
+        vm((4, 8, part, units), BF16),
         vm((half, units), F32),
-        vm((2, 8, part, units), BF16),
-        vm((7, 2, part, units), BF16),
-        vm((2, 7, part, units), BF16),
-        vm((2, 8, part, units), BF16),
-        vm((2, 2, 4, share, width), F32),
-        vm((2, 2, 4, share, width), BF16),
-        vm((2, 3, 2, share, width), BF16),
-        vm((2, 2, share, width), BF16),
-        vm((4, share, width), BF16),
+        vm((4, 8, part, units), BF16),
+        vm((7, 4, part, units), BF16),
+        vm((4, 7, part, units), BF16),
+        vm((4, 8, part, units), BF16),
+        vm((4, 2, 4, rows, width), F32),
+        vm((4, 2, 4, rows, width), BF16),
+        vm((4, 3, 2, rows, width), BF16),
+        vm((4, 2, rows, width), BF16),
+        vm((2, 4, rows, width), BF16),
         pltpu.SemaphoreType.REGULAR,
     ]
     scratch += [
         dma(n)
         for n in (
             (10,), (5,), (5,), (15,), (15,), (15,), (15,),
-            (7,), (7,), (2, 7), (2, 7), (2, 7), (2, 7), (2, 3), (2, 3), (2, 2), (4,),
+            (7,), (7,), (4, 7), (4, 7), (4, 7), (4, 7), (4, 3), (4, 3), (4, 2), (2, 4),
         )
     ]
     any_spec = pl.BlockSpec(memory_space=pl.ANY)

time: 42.3 us -> 41.4 us (0.979); the launches traced: 42.3 us -> 40.6 us
  Pallas kernels: 41.6 us -> 40 us
    pallas_call x1, Pallas kernels: 41.6 us -> 40 us  [shards(): pl.pallas_call(kernel, out_shape=jax.ShapeDtypeStruct((share, width), BF1...]
where the time goes in v7:
time: 41.4 us; the launch traced here: 40.6 us
  Pallas kernels  40 us (97%)
  local copies, waits for them, and re-layouts  0.62 us (1%)
    pallas_call x1, Pallas kernels, shards(): pl.pallas_call(kernel, out_shape=jax.ShapeDtypeStruct((share, width), BF1...  40 us

profile of v7, /device:TPU:1, one launch (start us, length us, event | category | flops | bytes accessed | tf_op | source)
XLA Modules:
  0.0 40.6 jit_solution(17683323981990690310)
XLA Ops:
  0.0 40.0 %shard_map.100 = bf16[32,256]{1,0:T(8,128)(2,1)S(1)} custom-call(bf16[256,2,256]{2,1,0:T(2,128)(2,1)} %tokens.1, bf16[512,1024]{1,0:T(8,128)(2,1)} %task_emb.1, bf16[1024,512]{1,0:T(8,128)(2,1)} %gen_in.1, bf16[256,512]{1,0:T(8,128)(2,1)} %bitcast.7, bf16[512,896]{1,0:T(8,128)(2,1)} %bitcast.6, bf16[256,896]{1,0:T(8,128)(2,1)} %w_gate.1, ...), custom_call_target="tpu_custom_call" | custom-call | tf_op jit(solution)/shard_map/pallas_call | solution.py:348
  40.0 0.6 %reshape.19 = bf16[16,2,256]{2,1,0:T(2,128)(2,1)} reshape(bf16[32,256]{1,0:T(8,128)(2,1)S(1)} %shard_map.100) | data formatting | bytes 32768 | tf_op jit(solution)/shard_map/reshape | solution.py:358

commit v8 on v7

--- a/solution.py
+++ b/solution.py
@@ -70,6 +70,9 @@
             src_ref=src, dst_ref=dst, send_sem=ss, recv_sem=rs, device_id=dev, device_id_type=MESH
         )
 
+    def all_of(ref, ss, rs):
+        return copy(ref, ref, ss, rs, (row, col))
+
     gi = lax.broadcasted_iota(jnp.int32, (groups, groups), 0)
     gj = lax.broadcasted_iota(jnp.int32, (groups, groups), 1)
     loads[0].wait()
@@ -88,27 +91,26 @@
 
     def member(first, width):
         m = lax.broadcasted_iota(jnp.int32, (groups, width), 1) + first
-        token = m // 64 % 4 * 128 + m // 16 % 4 * 32 + m // 256 * 16 + m % 16
-        request = (token // 2).astype(F32)
+        request = ((m >> 6 & 3) << 6) + ((m >> 4 & 3) << 4) + ((m >> 8) << 3) + ((m & 15) >> 1)
+        request = request.astype(F32)
         return jnp.where((request >= starts) & (request < ends), 1.0, 0.0)
 
     loads[4].wait()
     fac_a = dot(ga_v[...], hyper, ((1,), (1,))).astype(BF16)
-    half, width = tok_v.shape[1:]
+    half, width = tokp_v.shape[0] * tokp_v.shape[1], tokp_v.shape[2]
     n_tok = 2 * half
     slab = fac_a.shape[0] // ranks
     a_of = dot(fac_a, member(0, n_tok).astype(BF16))
-    which = lax.broadcasted_iota(jnp.int32, (slab * ranks, width), 0) // ranks + col * slab
+    which = (lax.broadcasted_iota(jnp.int32, (slab * ranks, width), 0) >> 4) + col * slab
     sel = jnp.where(lax.broadcasted_iota(jnp.int32, (slab * ranks, width), 1) == which, 1.0, 0.0)
     loads[5].wait()
-    tok = tok3_v[...].reshape(16, 2, n_tok // 32, width)
-    for k in range(2):
-        tok_v[k] = tok[:, k].reshape(half, width)
-    t_of = dot(sel.astype(BF16), tok_v[...].reshape(n_tok, width), ((1,), (1,)))
-    low = jnp.sum((a_of * t_of).reshape(slab, ranks, n_tok), axis=0)
+    tok_v[...] = tok3_v[...].reshape(tok_v.shape)
+    sel = sel.astype(BF16)
     for h in range(2):
+        t_of = dot(sel, tok_v[:, h].reshape(half, width), ((1,), (1,)))
+        low = jnp.sum((a_of[:, h * half : h * half + half] * t_of).reshape(slab, ranks, half), axis=0)
         for q in range(2):
-            low_s[h, :, q, :] = low[:, h * 256 + q * 128 : h * 256 + q * 128 + 128]
+            low_s[h, :, q, :] = low[:, q * 128 : q * 128 + 128]
 
     pl.semaphore_wait(bar, 21)
     for d in (2, 1, 3):
@@ -118,13 +120,13 @@
     for n, (dz, dy, dk) in enumerate(row_steps):
         to = in_row(dz, dy, dk)
         l1.append(
-            copy(low_s.at[to % 2, pl.ds(to // 2 * 2, 2)], low1_r.at[n], l1_ss.at[n], l1_rs.at[n], (to, col))
+            copy(low_s.at[to % 2, pl.ds(to // 2 * 2, 2)], low1_r.at[n], l1_ss, l1_rs, (to, col))
         )
         l1[-1].start()
     for n in (7, 8, 9):
         loads[n].wait()
     pair = [
-        copy(tok_v.at[1 - core], tokp_v, pair_ss.at[0], pair_rs.at[0], mate),
+        copy(tok_v.at[:, 1 - core], tokp_v, pair_ss.at[0], pair_rs.at[0], mate),
         copy(wg_v, wgp_v, pair_ss.at[1], pair_rs.at[1], mate),
         copy(wu_v, wup_v, pair_ss.at[2], pair_rs.at[2], mate),
         copy(wd_v, wdp_v, pair_ss.at[3], pair_rs.at[3], mate),
@@ -136,12 +138,13 @@
     b_v[core] = dot(hyper, gb_v[...]).astype(BF16)
     pair[4].start()
 
-    gate = dot(tok_v[core], wg_v[...])
+    tok = tok_v[:, core].reshape(half, width)
+    gate = dot(tok, wg_v[...])
     pair[0].wait_recv()
     pair[1].wait_recv()
     part = half // 32
     units = gate.shape[1]
-    gate_s[...] = (gate + dot(tokp_v[...], wgp_v[...])).astype(BF16).reshape(4, 8, part, units)
+    gate_s[...] = (gate + dot(tokp_v[...].reshape(half, width), wgp_v[...])).astype(BF16).reshape(4, 8, part, units)
 
     def peer(dz, dy, sign=1):
         return in_row(dz, dy, 0, sign) // 2
@@ -149,35 +152,33 @@
     gs = []
     for n, (dz, dy) in enumerate(chip_steps):
         i = peer(dz, dy)
-        gs.append(copy(gate_s.at[:, i], gate_r.at[n], g_ss.at[n], g_rs.at[n], (i * 2 + core, col)))
+        gs.append(copy(gate_s.at[:, i], gate_r.at[n], g_ss, g_rs, (i * 2 + core, col)))
     for n, (dz, dy) in enumerate(chip_steps):
         if dz == 0:
             gs[n].start()
 
     low = low_s[core, pl.ds(chip * 2, 2)]
-    for n in range(15):
-        l1[n].wait_recv()
-        low = low + low1_r[n]
+    all_of(low1_r, l1_ss, l1_rs).wait_recv()
+    low = low + jnp.sum(low1_r[...], axis=0)
     low2_s[...] = low
     pl.semaphore_wait(known, 3)
     l2 = []
     for n, (dz, dx) in enumerate(col_steps):
-        l2.append(copy(low2_s, low2_r.at[n], l2_ss.at[n], l2_rs.at[n], (row, in_col(dz, dx))))
+        l2.append(copy(low2_s, low2_r.at[n], l2_ss, l2_rs, (row, in_col(dz, dx))))
         l2[-1].start()
     for n, (dz, dy) in enumerate(chip_steps):
         if dz == 1:
             gs[n].start()
 
-    up = dot(tok_v[core], wu_v[...])
+    up = dot(tok, wu_v[...])
     pair[2].wait_recv()
-    up_f[...] = up + dot(tokp_v[...], wup_v[...])
+    up_f[...] = up + dot(tokp_v[...].reshape(half, width), wup_v[...])
     pair[4].wait_recv()
     b_all = b_v[...].reshape(2 * groups, units)
     block = half // 2
     mem = [member(core * half + a * block, block) for a in range(2)]
-    for n in range(15):
-        l2[n].wait_recv()
-        low = low + low2_r[n]
+    all_of(low2_r, l2_ss, l2_rs).wait_recv()
+    low = low + jnp.sum(low2_r[...], axis=0)
     low = low.astype(BF16).astype(F32)
     us = []
     for q in range(4):
@@ -185,7 +186,7 @@
         for n, (dz, dy) in enumerate(chip_steps):
             i = peer(dz, dy)
             us[q].append(
-                copy(up_s.at[q, i], up_r.at[q, n], u_ss.at[q, n], u_rs.at[q, n], (i * 2 + core, col))
+                copy(up_s.at[q, i], up_r.at[q, n], u_ss.at[q], u_rs.at[q], (i * 2 + core, col))
             )
     for a in range(2):
         spread = jnp.concatenate([mem[a] * low[r, a : a + 1, :] for r in range(2)], axis=0).astype(BF16)
@@ -195,25 +196,19 @@
             for c in us[q]:
                 c.start()
 
-    for n in range(7):
-        gs[n].wait_recv()
-    hs, ms, es = [], [], []
+    all_of(gate_r, g_ss, g_rs).wait_recv()
+    hs, ms = [], []
 
     def hidden(q):
-        gate = gate_s[q, chip].astype(F32)
-        for n in range(7):
-            gate = gate + gate_r[n, q].astype(F32)
-        act = jax.nn.silu(gate)
-        up = up_s[q, chip].astype(F32)
-        for n in range(7):
-            us[q][n].wait_recv()
-            up = up + up_r[q, n].astype(F32)
+        act = jax.nn.silu(gate_s[q, chip].astype(F32) + jnp.sum(gate_r[:, q].astype(F32), axis=0))
+        all_of(up_r.at[q], u_ss.at[q], u_rs.at[q]).wait_recv()
+        up = up_s[q, chip].astype(F32) + jnp.sum(up_r[q].astype(F32), axis=0)
         hid_v[q, chip] = (act * up).astype(BF16)
         hs.append([])
         for n, (dz, dy) in enumerate(chip_steps):
             hs[q].append(
                 copy(
-                    hid_v.at[q, chip], hid_v.at[q, chip], h_ss.at[q, n], h_rs.at[q, n],
+                    hid_v.at[q, chip], hid_v.at[q, chip], h_ss.at[q], h_rs.at[q],
                     (peer(dz, dy) * 2 + core, col),
                 )
             )
@@ -222,9 +217,7 @@
     rows = half // 16
 
     def partial(q):
-        for n, (dz, dy) in enumerate(chip_steps):
-            src = peer(dz, dy, -1)
-            copy(hid_v.at[q, src], hid_v.at[q, src], h_ss.at[q, n], h_rs.at[q, n], (row, col)).wait_recv()
+        all_of(hid_v.at[q, pl.ds(0, 7)], h_ss.at[q], h_rs.at[q]).wait_recv()
         hid = hid_v[q].reshape(8 * part, units)
         for k, w in enumerate((wd_v, wdp_v)):
             mix = dot(hid, w[...]).reshape(4, rows, width)
@@ -233,28 +226,23 @@
         ms.append([])
         for n, d in enumerate((2, 1, 3)):
             ms[q].append(
-                copy(mix_s.at[q, :, (x + d) % 4], mix_r.at[q, n], m_ss.at[q, n], m_rs.at[q, n], (row, in_col(0, d)))
+                copy(mix_s.at[q, :, (x + d) % 4], mix_r.at[q, n], m_ss.at[q], m_rs.at[q], (row, in_col(0, d)))
             )
             ms[q][-1].start()
 
     def end(q):
         here = z_hi == q
-        mix = mix_f[q, :, x]
-        for n in range(3):
-            ms[q][n].wait_recv()
-            mix = mix + mix_r[q, n].astype(F32)
-        end_s[q] = mix.astype(BF16)
+        all_of(mix_r.at[q], m_ss.at[q], m_rs.at[q]).wait_recv()
+        end_s[q] = (mix_f[q, :, x] + jnp.sum(mix_r[q].astype(F32), axis=0)).astype(BF16)
         slot = end_r.at[core, z_hi]
-        cross = copy(end_s.at[q, 1], slot, e_ss.at[q, 1], e_rs.at[core, z_hi], (mate[0], q * 4 + x))
-        same = copy(end_s.at[q, 0], slot, e_ss.at[q, 0], e_rs.at[core, z_hi], (row, q * 4 + x))
+        cross = copy(end_s.at[q, 1], slot, e_ss.at[1], e_rs.at[core], (mate[0], q * 4 + x))
+        same = copy(end_s.at[q, 0], slot, e_ss.at[0], e_rs.at[core], (row, q * 4 + x))
         pl.when(jnp.logical_not(here))(same.start)
         cross.start()
 
         @pl.when(here)
         def _():
             end_r[core, z_hi] = end_s[q, 0]
-
-        es.append((same, cross, here))
 
     hidden(0)
     for c in us[3]:
@@ -273,19 +261,22 @@
     end(3)
 
     for k in range(2):
-        for s in range(4):
-            arrived = copy(end_r.at[k, s], end_r.at[k, s], e_ss.at[0, 0], e_rs.at[k, s], (row, col))
-            pl.when(jnp.logical_not((core == k) & (z_hi == s)))(arrived.wait_recv)
-        total = end_r[k, 0].astype(F32)
-        for s in range(1, 4):
-            total = total + end_r[k, s].astype(F32)
+        pl.when(core == k)(all_of(end_r.at[k, pl.ds(0, 3)], e_ss.at[0], e_rs.at[k]).wait_recv)
+        pl.when(core != k)(all_of(end_r.at[k], e_ss.at[0], e_rs.at[k]).wait_recv)
+        total = jnp.sum(end_r[k].astype(F32), axis=0)
         out[k * rows : k * rows + rows, :] = total.astype(BF16)
 
-    for c in l1 + l2 + pair + gs + sum(us, []) + sum(hs, []) + sum(ms, []):
+    for c in pair:
         c.wait_send()
-    for same, cross, here in es:
-        pl.when(jnp.logical_not(here))(same.wait_send)
-        cross.wait_send()
+    all_of(low1_r, l1_ss, l1_rs).wait_send()
+    all_of(low2_r, l2_ss, l2_rs).wait_send()
+    all_of(gate_r, g_ss, g_rs).wait_send()
+    for q in range(4):
+        all_of(up_r.at[q], u_ss.at[q], u_rs.at[q]).wait_send()
+        all_of(hid_v.at[q, pl.ds(0, 7)], h_ss.at[q], h_rs.at[q]).wait_send()
+        all_of(mix_r.at[q], m_ss.at[q], m_rs.at[q]).wait_send()
+    all_of(end_s.at[pl.ds(0, 3), 0], e_ss.at[0], e_rs.at[0]).wait_send()
+    all_of(end_s.at[:, 1], e_ss.at[1], e_rs.at[0]).wait_send()
 
 
 def shards(tokens, task_emb, gen_in, gen_a, gen_b, w_gate, w_up, w_down, group_count, group_task):
@@ -314,8 +305,8 @@
     )
     scratch = [vm(a.shape, a.dtype) for a in args]
     scratch += [
-        vm((2, half, width), BF16),
-        vm((half, width), BF16),
+        vm((16, 2, rows, width), BF16),
+        vm((16, rows, width), BF16),
         vm((width, units), BF16),
         vm((width, units), BF16),
         vm((units, width), BF16),
@@ -337,13 +328,7 @@
         vm((2, 4, rows, width), BF16),
         pltpu.SemaphoreType.REGULAR,
     ]
-    scratch += [
-        dma(n)
-        for n in (
-            (10,), (5,), (5,), (15,), (15,), (15,), (15,),
-            (7,), (7,), (4, 7), (4, 7), (4, 7), (4, 7), (4, 3), (4, 3), (4, 2), (2, 4),
-        )
-    ]
+    scratch += [dma((10,)), dma((5,)), dma((5,))] + [dma] * 6 + [dma((4,))] * 6 + [dma((2,))] * 2
     any_spec = pl.BlockSpec(memory_space=pl.ANY)
     out = pl.pallas_call(
         kernel,

time: 41.4 us -> 39.6 us (0.957)
  the two profiles are of different devices: /device:TPU:1 before, /device:TPU:2 now
where the time goes in v8:
time: 39.6 us; the launch traced here: 39.5 us
  Pallas kernels  38.9 us (98%)
  local copies, waits for them, and re-layouts  0.62 us (2%)
    pallas_call x1, Pallas kernels, shards(): pl.pallas_call(kernel, out_shape=jax.ShapeDtypeStruct((share, width), BF1...  38.9 us

profile of v8, /device:TPU:2, one launch (start us, length us, event | category | flops | bytes accessed | tf_op | source)
XLA Modules:
  0.0 39.5 jit_solution(15893520563404253704)
XLA Ops:
  0.0 38.9 %shard_map.100 = bf16[32,256]{1,0:T(8,128)(2,1)S(1)} custom-call(bf16[256,2,256]{2,1,0:T(2,128)(2,1)} %tokens.1, bf16[512,1024]{1,0:T(8,128)(2,1)} %task_emb.1, bf16[1024,512]{1,0:T(8,128)(2,1)} %gen_in.1, bf16[256,512]{1,0:T(8,128)(2,1)} %bitcast.7, bf16[512,896]{1,0:T(8,128)(2,1)} %bitcast.6, bf16[256,896]{1,0:T(8,128)(2,1)} %w_gate.1, ...), custom_call_target="tpu_custom_call" | custom-call | tf_op jit(solution)/shard_map/pallas_call | solution.py:333
  38.9 0.6 %reshape.19 = bf16[16,2,256]{2,1,0:T(2,128)(2,1)} reshape(bf16[32,256]{1,0:T(8,128)(2,1)S(1)} %shard_map.100) | data formatting | bytes 32768 | tf_op jit(solution)/shard_map/reshape | solution.py:343

commit v9 on v8

--- a/solution.py
+++ b/solution.py
@@ -186,7 +186,7 @@
         for n, (dz, dy) in enumerate(chip_steps):
             i = peer(dz, dy)
             us[q].append(
-                copy(up_s.at[q, i], up_r.at[q, n], u_ss.at[q], u_rs.at[q], (i * 2 + core, col))
+                copy(up_s.at[q, i], up_r.at[q, n], u_ss, u_rs.at[q], (i * 2 + core, col))
             )
     for a in range(2):
         spread = jnp.concatenate([mem[a] * low[r, a : a + 1, :] for r in range(2)], axis=0).astype(BF16)
@@ -201,14 +201,14 @@
 
     def hidden(q):
         act = jax.nn.silu(gate_s[q, chip].astype(F32) + jnp.sum(gate_r[:, q].astype(F32), axis=0))
-        all_of(up_r.at[q], u_ss.at[q], u_rs.at[q]).wait_recv()
+        all_of(up_r.at[q], u_ss, u_rs.at[q]).wait_recv()
         up = up_s[q, chip].astype(F32) + jnp.sum(up_r[q].astype(F32), axis=0)
         hid_v[q, chip] = (act * up).astype(BF16)
         hs.append([])
         for n, (dz, dy) in enumerate(chip_steps):
             hs[q].append(
                 copy(
-                    hid_v.at[q, chip], hid_v.at[q, chip], h_ss.at[q], h_rs.at[q],
+                    hid_v.at[q, chip], hid_v.at[q, chip], h_ss, h_rs.at[q],
                     (peer(dz, dy) * 2 + core, col),
                 )
             )
@@ -217,7 +217,7 @@
     rows = half // 16
 
     def partial(q):
-        all_of(hid_v.at[q, pl.ds(0, 7)], h_ss.at[q], h_rs.at[q]).wait_recv()
+        all_of(hid_v.at[q, pl.ds(0, 7)], h_ss, h_rs.at[q]).wait_recv()
         hid = hid_v[q].reshape(8 * part, units)
         for k, w in enumerate((wd_v, wdp_v)):
             mix = dot(hid, w[...]).reshape(4, rows, width)
@@ -226,13 +226,13 @@
         ms.append([])
         for n, d in enumerate((2, 1, 3)):
             ms[q].append(
-                copy(mix_s.at[q, :, (x + d) % 4], mix_r.at[q, n], m_ss.at[q], m_rs.at[q], (row, in_col(0, d)))
+                copy(mix_s.at[q, :, (x + d) % 4], mix_r.at[q, n], m_ss, m_rs.at[q], (row, in_col(0, d)))
             )
             ms[q][-1].start()
 
     def end(q):
         here = z_hi == q
-        all_of(mix_r.at[q], m_ss.at[q], m_rs.at[q]).wait_recv()
+        all_of(mix_r.at[q], m_ss, m_rs.at[q]).wait_recv()
         end_s[q] = (mix_f[q, :, x] + jnp.sum(mix_r[q].astype(F32), axis=0)).astype(BF16)
         slot = end_r.at[core, z_hi]
         cross = copy(end_s.at[q, 1], slot, e_ss.at[1], e_rs.at[core], (mate[0], q * 4 + x))
@@ -253,10 +253,10 @@
     partial(0)
     hidden(3)
     partial(1)
+    partial(2)
     end(0)
-    partial(2)
+    partial(3)
     end(1)
-    partial(3)
     end(2)
     end(3)
 
@@ -271,10 +271,9 @@
     all_of(low1_r, l1_ss, l1_rs).wait_send()
     all_of(low2_r, l2_ss, l2_rs).wait_send()
     all_of(gate_r, g_ss, g_rs).wait_send()
-    for q in range(4):
-        all_of(up_r.at[q], u_ss.at[q], u_rs.at[q]).wait_send()
-        all_of(hid_v.at[q, pl.ds(0, 7)], h_ss.at[q], h_rs.at[q]).wait_send()
-        all_of(mix_r.at[q], m_ss.at[q], m_rs.at[q]).wait_send()
+    all_of(up_r, u_ss, u_rs.at[0]).wait_send()
+    all_of(hid_v.at[:, pl.ds(0, 7)], h_ss, h_rs.at[0]).wait_send()
+    all_of(mix_r, m_ss, m_rs.at[0]).wait_send()
     all_of(end_s.at[pl.ds(0, 3), 0], e_ss.at[0], e_rs.at[0]).wait_send()
     all_of(end_s.at[:, 1], e_ss.at[1], e_rs.at[0]).wait_send()
 
@@ -328,7 +327,7 @@
         vm((2, 4, rows, width), BF16),
         pltpu.SemaphoreType.REGULAR,
     ]
-    scratch += [dma((10,)), dma((5,)), dma((5,))] + [dma] * 6 + [dma((4,))] * 6 + [dma((2,))] * 2
+    scratch += [dma((10,)), dma((5,)), dma((5,))] + [dma] * 6 + [dma, dma((4,))] * 3 + [dma((2,))] * 2
     any_spec = pl.BlockSpec(memory_space=pl.ANY)
     out = pl.pallas_call(
         kernel,

time: 39.6 us -> 38.8 us (0.980)
  the two profiles are of different devices: /device:TPU:2 before, /device:TPU:1 now
where the time goes in v9:
time: 38.8 us; the launch traced here: 38.7 us
  Pallas kernels  38.1 us (98%)
  local copies, waits for them, and re-layouts  0.62 us (2%)
    pallas_call x1, Pallas kernels, shards(): pl.pallas_call(kernel, out_shape=jax.ShapeDtypeStruct((share, width), BF1...  38.1 us

profile of v9, /device:TPU:1, one launch (start us, length us, event | category | flops | bytes accessed | tf_op | source)
XLA Modules:
  0.0 38.7 jit_solution(17364354659576386611)
XLA Ops:
  0.0 38.1 %shard_map.100 = bf16[32,256]{1,0:T(8,128)(2,1)S(1)} custom-call(bf16[256,2,256]{2,1,0:T(2,128)(2,1)} %tokens.1, bf16[512,1024]{1,0:T(8,128)(2,1)} %task_emb.1, bf16[1024,512]{1,0:T(8,128)(2,1)} %gen_in.1, bf16[256,512]{1,0:T(8,128)(2,1)} %bitcast.7, bf16[512,896]{1,0:T(8,128)(2,1)} %bitcast.6, bf16[256,896]{1,0:T(8,128)(2,1)} %w_gate.1, ...), custom_call_target="tpu_custom_call" | custom-call | tf_op jit(solution)/shard_map/pallas_call | solution.py:332
  38.1 0.6 %reshape.19 = bf16[16,2,256]{2,1,0:T(2,128)(2,1)} reshape(bf16[32,256]{1,0:T(8,128)(2,1)S(1)} %shard_map.100) | data formatting | bytes 32768 | tf_op jit(solution)/shard_map/reshape | solution.py:342

commit v10 on v9

--- a/solution.py
+++ b/solution.py
@@ -43,7 +43,7 @@
 
     row_steps = [(dz, dy, dk) for dz in (1, 0) for dy in (2, 1, 3, 0) for dk in (1, 0)][:-1]
     col_steps = [(dz, dx) for dz in (2, 1, 3, 0) for dx in (2, 1, 3, 0)][:-1]
-    chip_steps = [(dz, dy) for dz in (1, 0) for dy in (2, 1, 3, 0)][:-1]
+    chip_steps = [(1, 2), (0, 2), (1, 1), (0, 1), (1, 3), (0, 3), (1, 0)]
 
     bar = pltpu.get_barrier_semaphore()
     for d in (2, 1, 3):
@@ -132,7 +132,7 @@
         copy(wd_v, wdp_v, pair_ss.at[3], pair_rs.at[3], mate),
         copy(b_v.at[core], b_v.at[core], pair_ss.at[4], pair_rs.at[4], mate),
     ]
-    for n in range(4):
+    for n in range(2):
         pair[n].start()
     loads[6].wait()
     b_v[core] = dot(hyper, gb_v[...]).astype(BF16)
@@ -169,6 +169,8 @@
     for n, (dz, dy) in enumerate(chip_steps):
         if dz == 1:
             gs[n].start()
+    pair[2].start()
+    pair[3].start()
 
     up = dot(tok, wu_v[...])
     pair[2].wait_recv()
@@ -188,11 +190,14 @@
             us[q].append(
                 copy(up_s.at[q, i], up_r.at[q, n], u_ss, u_rs.at[q], (i * 2 + core, col))
             )
-    for a in range(2):
-        spread = jnp.concatenate([mem[a] * low[r, a : a + 1, :] for r in range(2)], axis=0).astype(BF16)
-        up = up_f[a * block : a * block + block, :] + dot(spread, b_all, ((0,), (0,)))
-        up_s[2 * a : 2 * a + 2] = up.astype(BF16).reshape(2, 8, part, units)
-        for q in (0, 1) if a == 0 else (2,):
+    for q in range(4):
+        quarter = slice(q % 2 * 64, q % 2 * 64 + 64)
+        spread = jnp.concatenate(
+            [mem[q // 2][:, quarter] * low[r, q // 2 : q // 2 + 1, quarter] for r in range(2)], axis=0
+        ).astype(BF16)
+        up = up_f[q * 64 : q * 64 + 64, :] + dot(spread, b_all, ((0,), (0,)))
+        up_s[q] = up.astype(BF16).reshape(8, part, units)
+        if q < 3:
             for c in us[q]:
                 c.start()
 

time: 38.8 us -> 38.7 us (level)
  no operation moved by 1% of the time
where the time goes in v10:
time: 38.7 us
  Pallas kernels  38 us (98%)
  local copies, waits for them, and re-layouts  0.62 us (2%)
    pallas_call x1, Pallas kernels, shards(): pl.pallas_call(kernel, out_shape=jax.ShapeDtypeStruct((share, width), BF1...  38 us

profile of v10, /device:TPU:1, one launch (start us, length us, event | category | flops | bytes accessed | tf_op | source)
XLA Modules:
  0.0 38.7 jit_solution(1365465022760203646)
XLA Ops:
  0.0 38.0 %shard_map.100 = bf16[32,256]{1,0:T(8,128)(2,1)S(1)} custom-call(bf16[256,2,256]{2,1,0:T(2,128)(2,1)} %tokens.1, bf16[512,1024]{1,0:T(8,128)(2,1)} %task_emb.1, bf16[1024,512]{1,0:T(8,128)(2,1)} %gen_in.1, bf16[256,512]{1,0:T(8,128)(2,1)} %bitcast.7, bf16[512,896]{1,0:T(8,128)(2,1)} %bitcast.6, bf16[256,896]{1,0:T(8,128)(2,1)} %w_gate.1, ...), custom_call_target="tpu_custom_call" | custom-call | tf_op jit(solution)/shard_map/pallas_call | solution.py:337
  38.1 0.6 %reshape.19 = bf16[16,2,256]{2,1,0:T(2,128)(2,1)} reshape(bf16[32,256]{1,0:T(8,128)(2,1)S(1)} %shard_map.100) | data formatting | bytes 32768 | tf_op jit(solution)/shard_map/reshape | solution.py:347

commit v11 on v10

--- a/solution.py
+++ b/solution.py
@@ -197,9 +197,8 @@
         ).astype(BF16)
         up = up_f[q * 64 : q * 64 + 64, :] + dot(spread, b_all, ((0,), (0,)))
         up_s[q] = up.astype(BF16).reshape(8, part, units)
-        if q < 3:
-            for c in us[q]:
-                c.start()
+        for c in us[q]:
+            c.start()
 
     all_of(gate_r, g_ss, g_rs).wait_recv()
     hs, ms = [], []
@@ -250,8 +249,6 @@
             end_r[core, z_hi] = end_s[q, 0]
 
     hidden(0)
-    for c in us[3]:
-        c.start()
     hidden(1)
     hidden(2)
     pair[3].wait_recv()

time: 38.7 us -> 39.2 us (1.013)
  Pallas kernels: 38 us -> 38.5 us
    pallas_call x1, Pallas kernels: 38 us -> 38.5 us  [shards(): pl.pallas_call(kernel, out_shape=jax.ShapeDtypeStruct((share, width), BF1...]
where the time goes in v11:
time: 39.2 us; the launch traced here: 39.1 us
  Pallas kernels  38.5 us (98%)
  local copies, waits for them, and re-layouts  0.62 us (2%)
    pallas_call x1, Pallas kernels, shards(): pl.pallas_call(kernel, out_shape=jax.ShapeDtypeStruct((share, width), BF1...  38.5 us

profile of v11, /device:TPU:1, one launch (start us, length us, event | category | flops | bytes accessed | tf_op | source)
XLA Modules:
  0.0 39.1 jit_solution(18079546905661283850)
XLA Ops:
  0.0 38.5 %shard_map.100 = bf16[32,256]{1,0:T(8,128)(2,1)S(1)} custom-call(bf16[256,2,256]{2,1,0:T(2,128)(2,1)} %tokens.1, bf16[512,1024]{1,0:T(8,128)(2,1)} %task_emb.1, bf16[1024,512]{1,0:T(8,128)(2,1)} %gen_in.1, bf16[256,512]{1,0:T(8,128)(2,1)} %bitcast.7, bf16[512,896]{1,0:T(8,128)(2,1)} %bitcast.6, bf16[256,896]{1,0:T(8,128)(2,1)} %w_gate.1, ...), custom_call_target="tpu_custom_call" | custom-call | tf_op jit(solution)/shard_map/pallas_call | solution.py:334
  38.5 0.6 %reshape.19 = bf16[16,2,256]{2,1,0:T(2,128)(2,1)} reshape(bf16[32,256]{1,0:T(8,128)(2,1)S(1)} %shard_map.100) | data formatting | bytes 32768 | tf_op jit(solution)/shard_map/reshape | solution.py:344
